TPU v7x, 32 devices: a whole 2x2x4 slice. The times are simulated.
32 devices in a mesh: grp: 2 (over core), dev: 16 (over z, y, x).
Axes of the slice: x: 2, y: 2, z: 4, core: 2. Of those that a mesh axis runs over, the one named last changes fastest.
Arguments:
- pixel_tiles: float32 [2048, 6, 512], P(('grp', 'dev')), may hold values from -31 to 31
- blend_source: int32 [2048, 2], P(('grp', 'dev')), may hold values from 0 to 15, all different within a row; in each aligned block of 64 rows (0 to 63, 64 to 127, ...) at most 8 rows name the same one
- blend_slot: int32 [2048, 2], P(('grp', 'dev')), may hold values from 0 to 63
- component_count: int32 [2048], P(('grp', 'dev')), may hold values from 12 to 24
- sed_start: bfloat16 [2048, 24, 6], P(('grp', 'dev')), may hold values from 0.049804688 to 0.5
- morph_start: bfloat16 [2048, 2, 24, 512], P(('grp', 'dev')), may hold values from 0.019897461 to 0.5
Outputs:
- whitened: float32 [2048, 6, 512], P(('grp', 'dev'))
- sed_final: bfloat16 [2048, 24, 6], P(('grp', 'dev'))
Inputs may be any that keep to these rules, and one draw needn't show every extreme that they name: `blend_source`: each blend names 2 different devices of its region; over the blends of one device no device is named more than 8 times, and some device is named exactly 8 times. `blend_slot`: several blends may name the same tile.
All inputs are finite; a program needn't handle non-finite values.
Results may differ from a plain program's by a relative error of at most 0.0052.
Values may be sent and summed in bfloat16 or wider, within the bound.
A program may use at most 64 MiB of HBM per device.

v0:
```python
import functools
import math

import jax
import jax.numpy as jnp
from jax import lax
from jax.experimental import pallas as pl
from jax.experimental.pallas import tpu as pltpu
from jax.sharding import PartitionSpec as P

INWARD = 1
OUTWARD = 2
F32 = jnp.float32
BF16 = jnp.bfloat16
MESH = pl.DeviceIdType.MESH


def dot(a, b):
    return jnp.dot(a, b, preferred_element_type=F32)


def dot_nt(a, b):
    return lax.dot_general(a, b, (((1,), (1,)), ((), ())), preferred_element_type=F32)


def iota(shape, dimension):
    return lax.broadcasted_iota(jnp.int32, shape, dimension)


def split_row(shape, dimension, width):
    place = iota(shape, dimension)
    out = jnp.zeros(shape, jnp.int32)
    for cut in range(width, shape[dimension], width):
        out = out + (place >= cut).astype(jnp.int32)
    return out, place - out * width


def kernel(
    peers, regions, stride, size, tiles, source, slot, count, sed0, morph_hbm, white, sed_out, scale_out,
    morph_in, mor, tgt, mis, gram, seds, sed_b, sed_step, morph_step, mod, pt, ptt, req, wanted, send, arrived, outb, ret, part, parts,
    in_sem, ask_s, ask_r, put_s, put_r, back_s, back_r, sum_s, sum_r,
):
    bands, tile_rows, pixels = tiles.shape
    foot, rows = source.shape
    comps = sed0.shape[1]
    groups = rows // size
    slots = peers * stride
    me = lax.axis_index("dev")
    everyone = peers * regions
    my = lax.axis_index("grp") * peers + me
    load = pltpu.make_async_copy(morph_hbm, morph_in, in_sem)
    load.start()
    barrier = pltpu.get_barrier_semaphore()

    def greet(step, carry):
        other = lax.rem(my + step, everyone)
        pl.semaphore_signal(
            barrier, inc=1, device_id={"grp": lax.div(other, peers), "dev": lax.rem(other, peers)},
            device_id_type=MESH,
        )
        return carry

    lax.fori_loop(1, everyone, greet, 0)

    upper = (iota((rows, rows), 0) <= iota((rows, rows), 1)).astype(F32).astype(BF16)
    base = jnp.zeros((peers, 1), F32)
    want = jnp.zeros((slots, 1), F32)
    for f in range(foot):
        named = source[f : f + 1, :]
        hit = (iota((peers, rows), 0) == named).astype(F32)
        seen = dot(hit.astype(BF16), upper) + base
        rank = jnp.sum(hit * (seen - 1.0), axis=0, keepdims=True)
        base = base + jnp.sum(hit, axis=1, keepdims=True)
        place = named.astype(F32) * float(stride) + rank
        put = (iota((slots, rows), 0).astype(F32) == place).astype(F32)
        pt[f] = put.astype(BF16)
        ptt[f] = jnp.transpose(put).astype(BF16)
        want = want + jnp.sum(put * (slot[f : f + 1, :].astype(F32) + 1.0), axis=1, keepdims=True)
    req[...] = (
        jnp.broadcast_to(want, (slots, 128)).astype(jnp.int32).reshape(peers, stride, 128)
    )
    pl.semaphore_wait(barrier, everyone - 1)

    def exchange(src, dst, send_sem, recv_sem, lanes=None, at=None):
        def part_of(ref, index):
            return ref.at[index] if lanes is None else ref.at[index, :, lanes]

        def sem(ref, step):
            return ref.at[step] if at is None else ref.at[at, step]

        def copy(step, incoming):
            there = lax.rem(me + step, peers)
            here = lax.rem(me - step + peers, peers) if incoming else me
            return pltpu.make_async_remote_copy(
                src_ref=part_of(src, there), dst_ref=part_of(dst, here),
                send_sem=sem(send_sem, step), recv_sem=sem(recv_sem, step),
                device_id={"dev": there}, device_id_type=MESH,
            )

        def start():
            def body(step, carry):
                copy(step, False).start()
                return carry

            lax.fori_loop(1, peers, body, 0)

        def wait_in():
            def body(step, carry):
                copy(step, True).wait_recv()
                return carry

            lax.fori_loop(1, peers, body, 0)

        def wait_out():
            def body(step, carry):
                copy(step, False).wait_send()
                return carry

            lax.fori_loop(1, peers, body, 0)

        return start, wait_in, wait_out

    ask, ask_in, ask_out = exchange(req, wanted, ask_s, ask_r)
    ask()
    wanted[me] = req[me]

    width = size * comps
    span = size * bands
    blend_row, comp_row = split_row((width, 1), 0, comps)
    blend_col, comp_col = split_row((1, width), 1, comps)
    _, member_col = split_row((1, span), 1, size)
    band_row, member_row = split_row((span, 1), 0, size)
    same = (blend_row == blend_col).astype(F32)
    same_bd = (blend_row == member_col).astype(F32)
    same_t = (member_row == blend_col).astype(F32)
    gather_k = (iota((comps, width), 0) == comp_col).astype(F32).astype(BF16)
    sed_all = jnp.concatenate([sed0[b].astype(F32) for b in range(bands)], axis=1).astype(BF16)
    band_of, blend_of = split_row((1, bands * rows), 1, rows)
    counts = jnp.broadcast_to(count[...], (8, rows)).astype(F32).astype(BF16)
    pair = 2 if groups % 2 == 0 else 1

    def chosen(g):
        hit = (band_of == band_row) & (blend_of == g * size + member_row)
        return hit.astype(F32).astype(BF16)

    def norm(square, mask):
        flat = jnp.sum(square, axis=0, keepdims=True)
        return jnp.sqrt(jnp.sum(mask * flat, axis=1, keepdims=True)) + 1.0

    def wide(column):
        return jnp.broadcast_to(column, (column.shape[0], 128))

    def over_groups(body, pair=pair):
        def both(j, carry):
            stores = []
            for k in range(pair):
                stores = stores + body(j * pair + k)
            for ref, index, value in stores:
                ref[index] = value
            return carry

        lax.fori_loop(0, groups // pair, both, 0)

    load.wait()

    def begin(g):
        held = jnp.sum(
            jnp.where(iota((width, rows), 1) == g * size + blend_row, count[...], 0).astype(F32),
            axis=1, keepdims=True,
        )
        active = (comp_row.astype(F32) < held).astype(F32)
        owner = (iota((rows, width), 0) == g * size + blend_col).astype(F32).astype(BF16)
        active_t = (comp_col.astype(F32) < dot(counts, owner)[0:1]).astype(F32)
        first = dot_nt(chosen(g), sed_all)
        stores = [(seds, g, dot(first.astype(BF16), gather_k) * same_t * active_t)]
        for f in range(foot):
            whole = morph_in[pl.ds(g * size, size), f].astype(F32).reshape(width, pixels)
            stores.append((mor, (g, f), (whole * active).astype(BF16)))
        return stores

    over_groups(begin)
    ask_in()
    picks = (wanted[...].reshape(slots, 128)[:, :tile_rows] - 1 == iota((slots, tile_rows), 1)).astype(F32)
    pick = picks.astype(BF16)
    arrivals = INWARD if bands % INWARD == 0 else 1
    each = bands // arrivals
    fetches = []
    for c in range(arrivals):
        for b in range(c * each, (c + 1) * each):
            block = dot(pick, tiles[b].astype(BF16))
            send[:, :, b * pixels : (b + 1) * pixels] = block.reshape(
                peers, stride, pixels
            ).astype(BF16)
        lanes = slice(c * each * pixels, (c + 1) * each * pixels)
        fetches.append(exchange(send, arrived, put_s, put_r, lanes, c))
        fetches[-1][0]()
    arrived[me] = send[me]

    def grams_of(morphs):
        total = dot_nt(morphs[0], morphs[0])
        for f in range(1, foot):
            total = total + dot_nt(morphs[f], morphs[f])
        return total * same

    def cross_of(targets, morphs):
        total = dot_nt(targets[0], morphs[0])
        for f in range(1, foot):
            total = total + dot_nt(targets[f], morphs[f])
        return total

    def first_gram(g):
        total = grams_of([mor[g, f] for f in range(foot)])
        step = 1.0 / norm(total * total, same_t)
        return [(gram, g, total.astype(BF16)), (sed_step, g, wide(step))]

    over_groups(first_gram)

    for c in range(arrivals):
        fetches[c][1]()
        for b in range(c * each, (c + 1) * each):
            block = arrived[:, :, b * pixels : (b + 1) * pixels].astype(F32)
            block = block.reshape(slots, pixels).astype(BF16)
            for f in range(foot):
                tgt[:, f, b * size : (b + 1) * size, :] = dot(ptt[f], block).reshape(
                    groups, size, pixels
                )
        part_rows = slice(c * each * size, (c + 1) * each * size)

        def first_seds(g):
            targets = [tgt[g, f, part_rows] for f in range(foot)]
            morphs = [mor[g, f] for f in range(foot)]
            cross = cross_of([t.astype(BF16) for t in targets], morphs) * same_t[part_rows]
            old = seds[g, part_rows]
            slope = dot(old.astype(BF16), gram[g]) - cross
            sed = jnp.maximum(old - slope * sed_step[g, part_rows, 0:1], 0.0).astype(BF16)
            stores = [(seds, (g, part_rows), sed.astype(F32))]
            for f in range(foot):
                misfit = (dot(sed, morphs[f]) - targets[f]).astype(BF16)
                stores.append((mis, (g, f, part_rows), misfit))
            return stores

        over_groups(first_seds)

    def moved(morph, slope, step):
        return jnp.maximum(morph.astype(F32) - (slope + 0.1) * step, 0.0).astype(BF16)

    def morph_stepsize(sed):
        small = dot_nt(sed, sed)
        return 1.0 / norm(small * small, same_bd)

    def second_seds(g):
        old = seds[g]
        step = morph_stepsize(old.astype(BF16))
        lhs = jnp.transpose(old).astype(BF16)
        morphs = [moved(mor[g, f], dot(lhs, mis[g, f]), step) for f in range(foot)]
        stores = [(mor, (g, f), morphs[f]) for f in range(foot)]
        total = grams_of(morphs)
        cross = cross_of([tgt[g, f].astype(BF16) for f in range(foot)], morphs) * same_t
        slope = dot(old.astype(BF16), total.astype(BF16)) - cross
        sed = jnp.maximum(old - slope / norm(total * total, same_t), 0.0).astype(BF16)
        stores.append((seds, g, sed.astype(F32)))
        stores.append((sed_b, g, jnp.transpose(sed.astype(F32)).astype(BF16)))
        stores.append((morph_step, g, wide(morph_stepsize(sed))))
        return stores

    over_groups(second_seds)

    window = pixels // OUTWARD
    trips = []
    for chunk in range(OUTWARD):
        taken = slice(chunk * window, (chunk + 1) * window)

        def last_models(g):
            sed = seds[g].astype(BF16)
            stores = []
            for f in range(foot):
                morph = mor[g, f, :, taken]
                misfit = (dot(sed, morph) - tgt[g, f, :, taken]).astype(BF16)
                morph = moved(morph, dot(sed_b[g], misfit), morph_step[g, :, 0:1])
                model = dot(sed, morph).reshape(bands, size, window)
                member = pl.ds(pl.multiple_of(g * size, size), size)
                stores.append((mod, (f, slice(None), member, slice(None)), model))
            return stores

        over_groups(last_models)
        for b in range(bands):
            block = dot(pt[0], mod[0, b].astype(BF16))
            for f in range(1, foot):
                block = block + dot(pt[f], mod[f, b].astype(BF16))
            at = (chunk * bands + b) * window
            outb[:, :, at : at + window] = block.reshape(peers, stride, window).astype(BF16)
        lanes = slice(chunk * bands * window, (chunk + 1) * bands * window)
        trips.append(exchange(outb, ret, back_s, back_r, lanes, chunk))
        trips[-1][0]()
    ret[me] = outb[me]

    def place(g, placed):
        lean = dot_nt(gather_k, seds[g].astype(BF16))
        return placed + dot(lean.astype(BF16), chosen(g))

    placed = lax.fori_loop(0, groups, place, jnp.zeros((comps, bands * rows), F32))
    for b in range(bands):
        sed_out[b] = placed[:, b * rows : (b + 1) * rows].astype(BF16)
    pick_t = jnp.transpose(picks).astype(BF16)
    squares = jnp.zeros((8, 128), F32)
    for chunk in range(OUTWARD):
        trips[chunk][1]()
        taken = slice(chunk * window, (chunk + 1) * window)
        for b in range(bands):
            at = (chunk * bands + b) * window
            block = ret[:, :, at : at + window].astype(F32).reshape(slots, window).astype(BF16)
            residual = tiles[b, :, taken] - dot(pick_t, block)
            white[b, :, taken] = residual
            square = residual * residual
            for r in range(0, tile_rows, 8):
                for c in range(0, window, 128):
                    squares = squares + square[r : r + 8, c : c + 128]

    own_row = jnp.sum(squares, axis=0, keepdims=True)
    part[...] = own_row

    def share(step, incoming):
        there = lax.rem(my + step, everyone)
        here = lax.rem(my - step + everyone, everyone) if incoming else my
        return pltpu.make_async_remote_copy(
            src_ref=part, dst_ref=parts.at[here], send_sem=sum_s.at[step],
            recv_sem=sum_r.at[step],
            device_id={"grp": lax.div(there, peers), "dev": lax.rem(there, peers)}, device_id_type=MESH,
        )

    def start_share(step, carry):
        share(step, False).start()
        return carry

    def end_share(step, carry):
        share(step, True).wait_recv()
        return carry

    def end_sent(step, carry):
        share(step, False).wait_send()
        return carry

    lax.fori_loop(1, everyone, start_share, 0)
    parts[my] = own_row
    ask_out()
    for trip in fetches + trips:
        trip[2]()
    lax.fori_loop(1, everyone, end_share, 0)
    total = jnp.sum(parts[...], axis=0)
    total = jnp.sum(jnp.sum(total, axis=1, keepdims=True), axis=0, keepdims=True)
    count_all = float(bands * tile_rows * pixels * everyone)
    scale_out[...] = jnp.broadcast_to(1.0 / jnp.sqrt(total / count_all + 1e-06), (8, 128))
    lax.fori_loop(1, everyone, end_sent, 0)


def on_device(pixel_tiles, blend_source, blend_slot, component_count, sed_start, morph_start):
    peers = lax.axis_size("dev")
    regions = lax.axis_size("grp")
    rows, foot = blend_source.shape
    tile_rows, bands, pixels = pixel_tiles.shape
    comps = sed_start.shape[1]
    entries = rows * foot
    capacity = max(2, (entries + peers - 1) // peers)
    stride = (capacity + 7) // 8 * 8
    size = math.gcd(rows, 8)
    groups = rows // size
    slots = peers * stride
    flat = bands * pixels
    vmem = pl.BlockSpec(memory_space=pltpu.VMEM)
    dma = pltpu.SemaphoreType.DMA
    residual, sed_final, scale = pl.pallas_call(
        functools.partial(kernel, peers, regions, stride, size),
        out_shape=(
            jax.ShapeDtypeStruct((bands, tile_rows, pixels), F32),
            jax.ShapeDtypeStruct((bands, comps, rows), BF16),
            jax.ShapeDtypeStruct((8, 128), F32),
        ),
        in_specs=[vmem] * 5 + [pl.BlockSpec(memory_space=pl.ANY)],
        out_specs=(vmem, vmem, vmem),
        scratch_shapes=[
            pltpu.VMEM(morph_start.shape, BF16),
            pltpu.VMEM((groups, foot, size * comps, pixels), BF16),
            pltpu.VMEM((groups, foot, size * bands, pixels), F32),
            pltpu.VMEM((groups, foot, size * bands, pixels), BF16),
            pltpu.VMEM((groups, size * comps, size * comps), BF16),
            pltpu.VMEM((groups, size * bands, size * comps), F32),
            pltpu.VMEM((groups, size * comps, size * bands), BF16),
            pltpu.VMEM((groups, size * bands, 128), F32),
            pltpu.VMEM((groups, size * comps, 128), F32),
            pltpu.VMEM((foot, bands, rows, pixels // OUTWARD), F32),
            pltpu.VMEM((foot, slots, rows), BF16),
            pltpu.VMEM((foot, rows, slots), BF16),
            pltpu.VMEM((peers, stride, 128), jnp.int32),
            pltpu.VMEM((peers, stride, 128), jnp.int32),
            pltpu.VMEM((peers, stride, flat), BF16),
            pltpu.VMEM((peers, stride, flat), BF16),
            pltpu.VMEM((peers, stride, flat), BF16),
            pltpu.VMEM((peers, stride, flat), BF16),
            pltpu.VMEM((1, 128), F32),
            pltpu.VMEM((peers * regions, 1, 128), F32),
            dma,
            dma((peers,)),
            dma((peers,)),
            dma((INWARD, peers)),
            dma((INWARD, peers)),
            dma((OUTWARD, peers)),
            dma((OUTWARD, peers)),
            dma((peers * regions,)),
            dma((peers * regions,)),
        ],
        compiler_params=pltpu.CompilerParams(
            collective_id=0, has_side_effects=True, vmem_limit_bytes=60 * 1024 * 1024
        ),
    )(
        jnp.transpose(pixel_tiles, (1, 0, 2)),
        jnp.transpose(blend_source),
        jnp.transpose(blend_slot),
        component_count.reshape(1, rows),
        jnp.transpose(sed_start, (2, 1, 0)),
        morph_start,
    )
    white = residual * scale[0, 0]
    return jnp.transpose(white, (1, 0, 2)), jnp.transpose(sed_final, (2, 1, 0))


def solution(mesh):
    placed = (
        P(("grp", "dev"), None, None),
        P(("grp", "dev"), None),
        P(("grp", "dev"), None),
        P(("grp", "dev")),
        P(("grp", "dev"), None, None),
        P(("grp", "dev"), None, None, None),
    )
    return jax.shard_map(
        on_device,
        mesh=mesh,
        in_specs=placed,
        out_specs=(P(("grp", "dev"), None, None), P(("grp", "dev"), None, None)),
        check_vma=False,
    )
```

profile of v0, /device:TPU:0, one launch (start us, length us, event | category | flops | bytes accessed | tf_op | source)
XLA Modules:
  0.0 77.5 jit_solution(7134839931560537624)
XLA Ops:
  0.6 71.6 %shard_map.77 = (f32[6,64,512]{2,1,0:T(8,128)}, bf16[6,24,64]{2,1,0:T(8,128)(2,1)}, f32[8,128]{1,0:T(8,128)}) custom-call(f32[6,64,512]{2,1,0:T(8,128)} %bitcast.9, s32[2,64]{1,0:T(2,128)} %bitcast.12, s32[2,64]{1,0:T(2,128)} %bitcast.13, s32[1,64]{1,0:T(1,128)} %bitcast.14, bf16[6,24,64]{2,1,0:T(8,128)(2,1)} %bitcast.10, bf16[64,2,24,512]{3,2,1,0:T(8,128)(2,1)} %morph_hbm.1), custom_call_target="tpu_custom_call" | custom-call | tf_op jit(solution)/shard_map/pallas_call | solution.py:371
  72.2 1.2 %slice.3 = f32[1,1]{1,0:T(1,128)} slice(f32[8,128]{1,0:T(8,128)} %get-tuple-element.6), slice={[0:1], [0:1]} | slice | bytes 8 | tf_op jit(solution)/shard_map/slice | solution.py:422
  73.4 2.7 %multiply_bitcast_fusion = f32[64,6,512]{2,0,1:T(8,128)} fusion(f32[6,64,512]{2,1,0:T(8,128)} %get-tuple-element.5, f32[]{:T(128)} %bitcast.5), kind=kLoop, calls=%fused_computation | loop fusion | flops 196608 | bytes 1572868 | tf_op jit(solution)/shard_map/transpose | solution.py:423
  76.1 1.4 %copy.9 = bf16[64,24,6]{0,1,2:T(8,128)(2,1)} copy(bf16[64,24,6]{0,1,2:T(8,128)(2,1)} %bitcast.11) | data formatting | bytes 36864
where the time goes:
time: 77.8 us; the launch traced here: 77.5 us
  Pallas kernels  71.6 us (92%)
  other arithmetic  2.75 us (4%)
  local copies, waits for them, and re-layouts  2.57 us (3%)
    pallas_call x1, Pallas kernels, on_device(): pl.pallas_call(functools.partial(kernel, peers, regions, stride, size), o...  71.6 us
    transpose x1, other arithmetic, on_device(): jnp.transpose(white, (1, 0, 2))  2.75 us

commit v1 on v0

--- a/solution.py
+++ b/solution.py
@@ -35,9 +35,13 @@
     return out, place - out * width
 
 
+def tgt_depth(width, span):
+    return (width + span) // 16 * 16 + 16
+
+
 def kernel(
     peers, regions, stride, size, tiles, source, slot, count, sed0, morph_hbm, white, sed_out, scale_out,
-    morph_in, mor, tgt, mis, gram, seds, sed_b, sed_step, morph_step, mod, pt, ptt, req, wanted, send, arrived, outb, ret, part, parts,
+    morph_in, fit, gram, seds, sed_step, move, mod, pt, ptt, req, wanted, send, arrived, outb, ret, part, parts,
     in_sem, ask_s, ask_r, put_s, put_r, back_s, back_r, sum_s, sum_r,
 ):
     bands, tile_rows, pixels = tiles.shape
@@ -126,32 +130,39 @@
 
     width = size * comps
     span = size * bands
+    used = width + span
+    depth = tgt_depth(width, span)
     blend_row, comp_row = split_row((width, 1), 0, comps)
     blend_col, comp_col = split_row((1, width), 1, comps)
-    _, member_col = split_row((1, span), 1, size)
     band_row, member_row = split_row((span, 1), 0, size)
     same = (blend_row == blend_col).astype(F32)
-    same_bd = (blend_row == member_col).astype(F32)
     same_t = (member_row == blend_col).astype(F32)
+    members = (iota((size, width), 0) == blend_col).astype(F32)
+    unit = (iota((span, depth), 0) + width == iota((span, depth), 1)).astype(F32)
+    lift = (iota((size, depth), 1) == used).astype(F32)
     gather_k = (iota((comps, width), 0) == comp_col).astype(F32).astype(BF16)
     sed_all = jnp.concatenate([sed0[b].astype(F32) for b in range(bands)], axis=1).astype(BF16)
     band_of, blend_of = split_row((1, bands * rows), 1, rows)
     counts = jnp.broadcast_to(count[...], (8, rows)).astype(F32).astype(BF16)
-    pair = 2 if groups % 2 == 0 else 1
 
     def chosen(g):
         hit = (band_of == band_row) & (blend_of == g * size + member_row)
         return hit.astype(F32).astype(BF16)
 
-    def norm(square, mask):
-        flat = jnp.sum(square, axis=0, keepdims=True)
-        return jnp.sqrt(jnp.sum(mask * flat, axis=1, keepdims=True)) + 1.0
+    def every_band(column):
+        return jnp.concatenate([column] * bands, axis=0)
+
+    def sed_stepsize(total):
+        flat = jnp.sum(total * total, axis=0, keepdims=True)
+        return 1.0 / (jnp.sqrt(jnp.sum(members * flat, axis=1, keepdims=True)) + 1.0)
 
     def wide(column):
         return jnp.broadcast_to(column, (column.shape[0], 128))
 
-    def over_groups(body, pair=pair):
-        def both(j, carry):
+    def over_groups(body, pair):
+        pair = math.gcd(groups, pair)
+
+        def some(j, carry):
             stores = []
             for k in range(pair):
                 stores = stores + body(j * pair + k)
@@ -159,7 +170,7 @@
                 ref[index] = value
             return carry
 
-        lax.fori_loop(0, groups // pair, both, 0)
+        lax.fori_loop(0, groups // pair, some, 0)
 
     load.wait()
 
@@ -173,12 +184,14 @@
         active_t = (comp_col.astype(F32) < dot(counts, owner)[0:1]).astype(F32)
         first = dot_nt(chosen(g), sed_all)
         stores = [(seds, g, dot(first.astype(BF16), gather_k) * same_t * active_t)]
+        tail = (iota((depth - used, pixels), 0) == 0).astype(F32).astype(BF16)
         for f in range(foot):
             whole = morph_in[pl.ds(g * size, size), f].astype(F32).reshape(width, pixels)
-            stores.append((mor, (g, f), (whole * active).astype(BF16)))
+            stores.append((fit, (g, f, slice(0, width)), (whole * active).astype(BF16)))
+            stores.append((fit, (g, f, slice(used, depth)), tail))
         return stores
 
-    over_groups(begin)
+    over_groups(begin, 2)
     ask_in()
     picks = (wanted[...].reshape(slots, 128)[:, :tile_rows] - 1 == iota((slots, tile_rows), 1)).astype(F32)
     pick = picks.astype(BF16)
@@ -196,24 +209,17 @@
         fetches[-1][0]()
     arrived[me] = send[me]
 
-    def grams_of(morphs):
-        total = dot_nt(morphs[0], morphs[0])
+    def morph_of(g, f):
+        return fit[g, f, 0:width]
+
+    def first_gram(g):
+        total = dot_nt(morph_of(g, 0), morph_of(g, 0))
         for f in range(1, foot):
-            total = total + dot_nt(morphs[f], morphs[f])
-        return total * same
-
-    def cross_of(targets, morphs):
-        total = dot_nt(targets[0], morphs[0])
-        for f in range(1, foot):
-            total = total + dot_nt(targets[f], morphs[f])
-        return total
-
-    def first_gram(g):
-        total = grams_of([mor[g, f] for f in range(foot)])
-        step = 1.0 / norm(total * total, same_t)
-        return [(gram, g, total.astype(BF16)), (sed_step, g, wide(step))]
-
-    over_groups(first_gram)
+            total = total + dot_nt(morph_of(g, f), morph_of(g, f))
+        total = total * same
+        return [(gram, g, total.astype(BF16)), (sed_step, g, wide(sed_stepsize(total)))]
+
+    over_groups(first_gram, 2)
 
     for c in range(arrivals):
         fetches[c][1]()
@@ -221,49 +227,56 @@
             block = arrived[:, :, b * pixels : (b + 1) * pixels].astype(F32)
             block = block.reshape(slots, pixels).astype(BF16)
             for f in range(foot):
-                tgt[:, f, b * size : (b + 1) * size, :] = dot(ptt[f], block).reshape(
-                    groups, size, pixels
+                at = width + b * size
+                fit[:, f, at : at + size, :] = (
+                    dot(ptt[f], block).astype(BF16).reshape(groups, size, pixels)
                 )
-        part_rows = slice(c * each * size, (c + 1) * each * size)
-
-        def first_seds(g):
-            targets = [tgt[g, f, part_rows] for f in range(foot)]
-            morphs = [mor[g, f] for f in range(foot)]
-            cross = cross_of([t.astype(BF16) for t in targets], morphs) * same_t[part_rows]
-            old = seds[g, part_rows]
-            slope = dot(old.astype(BF16), gram[g]) - cross
-            sed = jnp.maximum(old - slope * sed_step[g, part_rows, 0:1], 0.0).astype(BF16)
-            stores = [(seds, (g, part_rows), sed.astype(F32))]
-            for f in range(foot):
-                misfit = (dot(sed, morphs[f]) - targets[f]).astype(BF16)
-                stores.append((mis, (g, f, part_rows), misfit))
-            return stores
-
-        over_groups(first_seds)
-
-    def moved(morph, slope, step):
-        return jnp.maximum(morph.astype(F32) - (slope + 0.1) * step, 0.0).astype(BF16)
-
-    def morph_stepsize(sed):
-        small = dot_nt(sed, sed)
-        return 1.0 / norm(small * small, same_bd)
+
+    def first_seds(g):
+        cross = dot_nt(fit[g, 0, width:used], morph_of(g, 0))
+        for f in range(1, foot):
+            cross = cross + dot_nt(fit[g, f, width:used], morph_of(g, f))
+        old = seds[g]
+        slope = dot(old.astype(BF16), gram[g]) - cross * same_t
+        sed = jnp.maximum(old - slope * every_band(sed_step[g, :, 0:1]), 0.0).astype(BF16)
+        return [(seds, g, sed.astype(F32))]
+
+    def plan_move(g):
+        sed = seds[g]
+        held = sed.astype(BF16)
+        small = dot_nt(held, held)
+        flat = jnp.sum(small * small, axis=1, keepdims=True).reshape(bands, size, 1)
+        step = 1.0 / (jnp.sqrt(jnp.sum(flat, axis=0)) + 1.0)
+        blank = jnp.zeros((span, depth - width), F32)
+        right = (unit - jnp.concatenate([sed, blank], axis=1)) * every_band(step)
+        right = jnp.concatenate([right, lift * (-0.1 * step)], axis=0).astype(BF16)
+        left = jnp.transpose(jnp.concatenate([sed, members], axis=0)).astype(BF16)
+        return [(move, g, dot(left, right).astype(BF16))]
+
+    def moved(g, f, lanes):
+        shift = dot(move[g], fit[g, f, :, lanes])
+        return jnp.maximum(fit[g, f, 0:width, lanes].astype(F32) + shift, 0.0).astype(BF16)
+
+    def first_morphs(g):
+        lanes = slice(0, pixels)
+        return [(fit, (g, f, slice(0, width)), moved(g, f, lanes)) for f in range(foot)]
 
     def second_seds(g):
+        total = dot_nt(fit[g, 0, 0:used], morph_of(g, 0))
+        for f in range(1, foot):
+            total = total + dot_nt(fit[g, f, 0:used], morph_of(g, f))
+        cross = total[width:used] * same_t
+        total = total[0:width] * same
         old = seds[g]
-        step = morph_stepsize(old.astype(BF16))
-        lhs = jnp.transpose(old).astype(BF16)
-        morphs = [moved(mor[g, f], dot(lhs, mis[g, f]), step) for f in range(foot)]
-        stores = [(mor, (g, f), morphs[f]) for f in range(foot)]
-        total = grams_of(morphs)
-        cross = cross_of([tgt[g, f].astype(BF16) for f in range(foot)], morphs) * same_t
         slope = dot(old.astype(BF16), total.astype(BF16)) - cross
-        sed = jnp.maximum(old - slope / norm(total * total, same_t), 0.0).astype(BF16)
-        stores.append((seds, g, sed.astype(F32)))
-        stores.append((sed_b, g, jnp.transpose(sed.astype(F32)).astype(BF16)))
-        stores.append((morph_step, g, wide(morph_stepsize(sed))))
-        return stores
-
-    over_groups(second_seds)
+        sed = jnp.maximum(old - slope * every_band(sed_stepsize(total)), 0.0).astype(BF16)
+        return [(seds, g, sed.astype(F32))]
+
+    over_groups(first_seds, 4)
+    over_groups(plan_move, 4)
+    over_groups(first_morphs, 2)
+    over_groups(second_seds, 4)
+    over_groups(plan_move, 4)
 
     window = pixels // OUTWARD
     trips = []
@@ -274,15 +287,12 @@
             sed = seds[g].astype(BF16)
             stores = []
             for f in range(foot):
-                morph = mor[g, f, :, taken]
-                misfit = (dot(sed, morph) - tgt[g, f, :, taken]).astype(BF16)
-                morph = moved(morph, dot(sed_b[g], misfit), morph_step[g, :, 0:1])
-                model = dot(sed, morph).reshape(bands, size, window)
+                model = dot(sed, moved(g, f, taken)).reshape(bands, size, window)
                 member = pl.ds(pl.multiple_of(g * size, size), size)
                 stores.append((mod, (f, slice(None), member, slice(None)), model))
             return stores
 
-        over_groups(last_models)
+        over_groups(last_models, 2)
         for b in range(bands):
             block = dot(pt[0], mod[0, b].astype(BF16))
             for f in range(1, foot):
@@ -366,6 +376,7 @@
     groups = rows // size
     slots = peers * stride
     flat = bands * pixels
+    depth = tgt_depth(size * comps, size * bands)
     vmem = pl.BlockSpec(memory_space=pltpu.VMEM)
     dma = pltpu.SemaphoreType.DMA
     residual, sed_final, scale = pl.pallas_call(
@@ -379,14 +390,11 @@
         out_specs=(vmem, vmem, vmem),
         scratch_shapes=[
             pltpu.VMEM(morph_start.shape, BF16),
-            pltpu.VMEM((groups, foot, size * comps, pixels), BF16),
-            pltpu.VMEM((groups, foot, size * bands, pixels), F32),
-            pltpu.VMEM((groups, foot, size * bands, pixels), BF16),
+            pltpu.VMEM((groups, foot, depth, pixels), BF16),
             pltpu.VMEM((groups, size * comps, size * comps), BF16),
             pltpu.VMEM((groups, size * bands, size * comps), F32),
-            pltpu.VMEM((groups, size * comps, size * bands), BF16),
-            pltpu.VMEM((groups, size * bands, 128), F32),
-            pltpu.VMEM((groups, size * comps, 128), F32),
+            pltpu.VMEM((groups, size, 128), F32),
+            pltpu.VMEM((groups, size * comps, depth), BF16),
             pltpu.VMEM((foot, bands, rows, pixels // OUTWARD), F32),
             pltpu.VMEM((foot, slots, rows), BF16),
             pltpu.VMEM((foot, rows, slots), BF16),

time: 77.8 us -> 74 us (0.951)
  Pallas kernels: 71.6 us -> 67.8 us
    pallas_call x1, Pallas kernels: 71.6 us -> 67.8 us  [on_device(): pl.pallas_call(functools.partial(kernel, peers, regions, stride, size), o...]
where the time goes in v1:
time: 74 us; the launch traced here: 73.7 us
  Pallas kernels  67.8 us (92%)
  other arithmetic  2.75 us (4%)
  local copies, waits for them, and re-layouts  2.57 us (3%)
    pallas_call x1, Pallas kernels, on_device(): pl.pallas_call(functools.partial(kernel, peers, regions, stride, size), o...  67.8 us
    transpose x1, other arithmetic, on_device(): jnp.transpose(white, (1, 0, 2))  2.75 us

profile of v1, /device:TPU:0, one launch (start us, length us, event | category | flops | bytes accessed | tf_op | source)
XLA Modules:
  0.0 73.7 jit_solution(16718286808905909212)
XLA Ops:
  0.6 67.8 %shard_map.77 = (f32[6,64,512]{2,1,0:T(8,128)}, bf16[6,24,64]{2,1,0:T(8,128)(2,1)}, f32[8,128]{1,0:T(8,128)}) custom-call(f32[6,64,512]{2,1,0:T(8,128)} %bitcast.9, s32[2,64]{1,0:T(2,128)} %bitcast.12, s32[2,64]{1,0:T(2,128)} %bitcast.13, s32[1,64]{1,0:T(1,128)} %bitcast.14, bf16[6,24,64]{2,1,0:T(8,128)(2,1)} %bitcast.10, bf16[64,2,24,512]{3,2,1,0:T(8,128)(2,1)} %morph_hbm.1), custom_call_target="tpu_custom_call" | custom-call | tf_op jit(solution)/shard_map/pallas_call | solution.py:382
  68.4 1.2 %slice.3 = f32[1,1]{1,0:T(1,128)} slice(f32[8,128]{1,0:T(8,128)} %get-tuple-element.6), slice={[0:1], [0:1]} | slice | bytes 8 | tf_op jit(solution)/shard_map/slice | solution.py:430
  69.6 2.7 %multiply_bitcast_fusion = f32[64,6,512]{2,0,1:T(8,128)} fusion(f32[6,64,512]{2,1,0:T(8,128)} %get-tuple-element.5, f32[]{:T(128)} %bitcast.5), kind=kLoop, calls=%fused_computation | loop fusion | flops 196608 | bytes 1572868 | tf_op jit(solution)/shard_map/transpose | solution.py:431
  72.3 1.4 %copy.9 = bf16[64,24,6]{0,1,2:T(8,128)(2,1)} copy(bf16[64,24,6]{0,1,2:T(8,128)(2,1)} %bitcast.11) | data formatting | bytes 36864

commit v2 on v1

v2 whole, which is shorter than its diff:
```python
import functools
import math

import jax
import jax.numpy as jnp
from jax import lax
from jax.experimental import pallas as pl
from jax.experimental.pallas import tpu as pltpu
from jax.sharding import PartitionSpec as P

F32 = jnp.float32
BF16 = jnp.bfloat16
MESH = pl.DeviceIdType.MESH


def dot(a, b):
    return jnp.dot(a, b, preferred_element_type=F32)


def dot_nt(a, b):
    return lax.dot_general(a, b, (((1,), (1,)), ((), ())), preferred_element_type=F32)


def iota(shape, dimension):
    return lax.broadcasted_iota(jnp.int32, shape, dimension)


def count_up(shape, dimension):
    return iota(shape, dimension).astype(F32)


def split_row(shape, dimension, width):
    place = iota(shape, dimension)
    out = jnp.zeros(shape, jnp.int32)
    for cut in range(width, shape[dimension], width):
        out = out + (place >= cut).astype(jnp.int32)
    return out, place - out * width


def flag(condition):
    return condition.astype(F32)


def lanes_of(*parts):
    return parts[0] if len(parts) == 1 else jnp.concatenate(parts, axis=1)


def rows_of(*parts):
    return parts[0] if len(parts) == 1 else jnp.concatenate(parts, axis=0)


def tgt_depth(width, span):
    return (width + span) // 16 * 16 + 16


def plan_slots(peers, rows, foot, bands, groups):
    entries = rows * foot
    capacity = max(2, (entries + peers - 1) // peers)
    even = foot == 2 and peers * capacity == entries and capacity % 4 == 0
    halves = 2 if even and groups % 2 == 0 and entries == 128 else 1
    held = capacity // halves
    while held * bands % 8:
        held = held + 1
    return halves, held


def partners(col, row, before, after):
    alike = flag(col == row)
    rank_col = jnp.sum(alike * before, axis=1, keepdims=True)
    rank_row = jnp.sum(alike * after, axis=0, keepdims=True)
    level = flag(jnp.floor(rank_col * 0.5) == jnp.floor(rank_row * 0.5))
    return alike * level * (before + after)


def halve(source_col, source_row, n):
    entries = 2 * n
    before = flag(iota((entries, entries), 1) < iota((entries, entries), 0))
    after = flag(iota((entries, entries), 1) > iota((entries, entries), 0))
    pair = partners(source_col, source_row, before, after)
    step = rows_of(pair[n:], pair[:n]).astype(BF16)
    least = count_up((entries, entries), 0)
    reach = 1
    while reach < n:
        both = dot(step, lanes_of(step, least.astype(BF16)))
        least = jnp.minimum(least, both[:, entries:])
        step = both[:, :entries].astype(BF16)
        reach = reach * 2
    tail = (least[:n] < least[n:])[:, 0:1]
    tail_col = jnp.where(tail, source_col[:n], source_col[n:])
    head_col = jnp.where(tail, source_col[n:], source_col[:n])
    lane = iota((n, 128), 1)
    turned = jnp.transpose(jnp.where(lane == 0, tail_col, jnp.where(lane == 1, head_col, 0.0)))
    before = before[:n, :n]
    after = after[:n, :n]
    tails = partners(tail_col, turned[0:1], before, after).astype(BF16)
    heads = partners(head_col, turned[1:2], before, after).astype(BF16)
    step = dot(tails, heads).astype(BF16)
    least = count_up((n, n), 0)
    reach = 1
    while reach < n // 2:
        least = jnp.minimum(least, dot(step, least.astype(BF16)))
        step = dot(step, step).astype(BF16)
        reach = reach * 2
    return flag(least >= dot(tails, least.astype(BF16)))


def kernel(
    peers, regions, halves, held, size, tiles_hbm, source, slot, count, sed0, morph_hbm, white, sed_out, scale_out,
    tiles, tiles_b, morph_in, fit, gram, seds, sed_step, move, mod, order_v, order_s, req, wanted, send, arrived, outb, ret, part, parts,
    in_sem, ask_s, ask_r, put_s, put_r, back_s, back_r, sum_s, sum_r,
):
    bands, tile_rows, pixels = tiles.shape
    foot, rows = source.shape
    comps = sed0.shape[1]
    groups = rows // size
    per_half = groups // halves
    me = lax.axis_index("dev")
    everyone = peers * regions
    my = lax.axis_index("grp") * peers + me
    load_tiles = pltpu.make_async_copy(tiles_hbm, tiles, in_sem.at[0])
    load_tiles.start()
    load = pltpu.make_async_copy(morph_hbm, morph_in, in_sem.at[1])
    load.start()
    barrier = pltpu.get_barrier_semaphore()

    def greet(step, carry):
        other = lax.rem(my + step, everyone)
        pl.semaphore_signal(
            barrier, inc=1, device_id={"grp": lax.div(other, peers), "dev": lax.rem(other, peers)},
            device_id_type=MESH,
        )
        return carry

    lax.fori_loop(1, everyone, greet, 0)

    entries = foot * rows
    source_row = lanes_of(*[source[f : f + 1, :] for f in range(foot)]).astype(F32)
    slot_row = lanes_of(*[slot[f : f + 1, :] for f in range(foot)]).astype(F32)
    turned = jnp.transpose(rows_of(source_row, slot_row, jnp.zeros((6, entries), F32)))
    source_col = turned[:, 0:1]
    slot_col = turned[:, 1:2]
    before = flag(iota((entries, entries), 1) < iota((entries, entries), 0))
    after = flag(iota((entries, entries), 1) > iota((entries, entries), 0))
    alike = flag(source_col == source_row)
    if halves == 2:
        half = halve(source_col, source_row, rows)
        half_col = half[:, 0:1]
        half_row = jnp.transpose(lanes_of(half, half))[0:1]
        alone = flag(half_col == half_row)
        base = rows // 2
        pos_col = half_col * base + jnp.sum(alone * before[:rows, :rows], axis=1, keepdims=True)
        pos_row = half_row * base + jnp.sum(alone * after[:rows, :rows], axis=0, keepdims=True)
        both_col = rows_of(half_col, half_col)
        both_row = lanes_of(half_row, half_row)
        alike = alike * flag(both_col == both_row)
        rank_col = jnp.sum(alike * before, axis=1, keepdims=True)
        rank_row = jnp.sum(alike * after, axis=0, keepdims=True)
        lane_col = both_col * held + rank_col
    else:
        pos_col = count_up((rows, 1), 0)
        pos_row = count_up((1, rows), 1)
        rank_col = jnp.sum(alike * before, axis=1, keepdims=True)
        rank_row = jnp.sum(alike * after, axis=0, keepdims=True)
        lane_col = rank_col
    named = flag(count_up((peers, entries), 0) == source_row)
    asked = flag(count_up((entries, 128), 1) == lane_col) * (slot_col + 1.0)
    req[...] = dot(named.astype(BF16), asked.astype(BF16)).reshape(peers, 1, 128)
    pl.semaphore_wait(barrier, everyone - 1)

    def exchange(src, dst, send_sem, recv_sem):
        def copy(step, incoming):
            there = lax.rem(me + step, peers)
            here = lax.rem(me - step + peers, peers) if incoming else me
            return pltpu.make_async_remote_copy(
                src_ref=src.at[there], dst_ref=dst.at[here],
                send_sem=send_sem.at[step], recv_sem=recv_sem.at[step],
                device_id={"dev": there}, device_id_type=MESH,
            )

        def start():
            def body(step, carry):
                copy(step, False).start()
                return carry

            lax.fori_loop(1, peers, body, 0)

        def wait_in():
            def body(step, carry):
                copy(step, True).wait_recv()
                return carry

            lax.fori_loop(1, peers, body, 0)

        def wait_out():
            def body(step, carry):
                copy(step, False).wait_send()
                return carry

            lax.fori_loop(1, peers, body, 0)

        return start, wait_in, wait_out

    ask, ask_in, ask_out = exchange(req, wanted, ask_s, ask_r)
    ask()
    wanted[me] = req[me]

    order = jnp.sum(flag(count_up((rows, 128), 1) == pos_col) * count_up((rows, 128), 0), axis=0, keepdims=True)
    order = jnp.minimum(order, float(rows - 1))
    order_v[...] = jnp.broadcast_to(order, (8, 128)).astype(jnp.int32)
    to_scalars = pltpu.make_async_copy(order_v, order_s, in_sem.at[2])
    to_scalars.start()

    width = size * comps
    span = size * bands
    used = width + span
    depth = tgt_depth(width, span)
    blend_row, comp_row = split_row((width, 1), 0, comps)
    blend_col, comp_col = split_row((1, width), 1, comps)
    band_row, member_row = split_row((span, 1), 0, size)
    same = flag(blend_row == blend_col)
    same_t = flag(member_row == blend_col)
    members = flag(iota((size, width), 0) == blend_col)
    unit = flag(iota((span, depth), 0) + width == iota((span, depth), 1))
    lift = flag(iota((size, depth), 1) == used)
    eye = flag(iota((width, width), 0) == iota((width, width), 1)).astype(BF16)
    gather_k = flag(iota((comps, width), 0) == comp_col).astype(BF16)
    sed_all = jnp.concatenate([sed0[b].astype(F32) for b in range(bands)], axis=1).astype(BF16)
    band_of, _ = split_row((1, bands * rows), 1, rows)
    pos_of = lanes_of(*[pos_row] * bands)
    counts = jnp.broadcast_to(count[...], (8, rows)).astype(F32).astype(BF16)

    def chosen(g):
        hit = (band_of == band_row) & (pos_of == (g * size + member_row).astype(F32))
        return flag(hit).astype(BF16)

    def every_band(column):
        return jnp.concatenate([column] * bands, axis=0)

    def sed_stepsize(total):
        flat = jnp.sum(total * total, axis=0, keepdims=True)
        return 1.0 / (jnp.sqrt(jnp.sum(members * flat, axis=1, keepdims=True)) + 1.0)

    def wide(column):
        return jnp.broadcast_to(column, (column.shape[0], 128))

    def over_groups(body, first, number, pair):
        pair = math.gcd(number, pair)

        def some(j, carry):
            stores = []
            for k in range(pair):
                stores = stores + body(first + j * pair + k)
            for ref, index, value in stores:
                ref[index] = value
            return carry

        lax.fori_loop(0, number // pair, some, 0)

    to_scalars.wait()
    load.wait()

    def begin(g):
        mine = pos_row == (g * size + blend_row).astype(F32)
        kept = jnp.sum(jnp.where(mine, count[...].astype(F32), 0.0), axis=1, keepdims=True)
        active = flag(comp_row.astype(F32) < kept)
        owner = flag(pos_col == (g * size + blend_col).astype(F32)).astype(BF16)
        active_t = flag(comp_col.astype(F32) < dot(counts, owner)[0:1])
        first = dot_nt(chosen(g), sed_all)
        stores = [(seds, g, dot(first.astype(BF16), gather_k) * same_t * active_t)]
        tail = flag(iota((depth - used, pixels), 0) == 0).astype(BF16)
        places = [jnp.clip(order_s[0, g * size + m], 0, rows - 1) for m in range(size)]
        for f in range(foot):
            whole = rows_of(*[morph_in[place, f].astype(F32) for place in places])
            stores.append((fit, (g, f, slice(0, width)), (whole * active).astype(BF16)))
            stores.append((fit, (g, f, slice(used, depth)), tail))
        return stores

    over_groups(begin, 0, groups, 2)
    load_tiles.wait()
    tiles_b[...] = tiles[...].reshape(bands * tile_rows, pixels).astype(BF16)

    team = math.gcd(peers, 16)
    each = bands * held
    crowd = team * each
    stock = bands * tile_rows
    teams = [slice(k, k + team) for k in range(0, peers, team)]
    _, seat_row = split_row((crowd, 1), 0, each)
    seat_band_row, seat_rank_row = split_row((crowd, 1), 0, held)
    peer_col, seat_col = split_row((1, crowd), 1, each)
    seat_band_row = seat_band_row - split_row((crowd, 1), 0, each)[0] * bands
    seat_band_col, seat_rank_col = split_row((1, crowd), 1, held)
    seat_band_col = seat_band_col - peer_col * bands

    def pick_of(h, who):
        lines = jnp.broadcast_to(wanted[who], (team, each, 128)).reshape(crowd, 128)
        seat = flag(iota((crowd, 128), 1) == h * held + seat_rank_row)
        tile = jnp.sum(lines * seat, axis=1, keepdims=True)
        at = jnp.where(tile > 0.0, tile - 1.0 + (seat_band_row * tile_rows).astype(F32), -1.0)
        return flag(count_up((crowd, stock), 1) == at).astype(BF16)

    def pick_t_of(h, who):
        lines = wanted[who].reshape(team, 128).astype(BF16)
        seat = flag(iota((128, crowd), 0) == h * held + seat_rank_col).astype(BF16)
        tile = dot(lines, seat) * flag(iota((team, crowd), 0) == peer_col)
        tile = jnp.sum(tile, axis=0, keepdims=True)
        at = jnp.where(tile > 0.0, tile - 1.0 + (seat_band_col * tile_rows).astype(F32), -1.0)
        return flag(count_up((stock, crowd), 0) == at).astype(BF16)

    ask_in()
    fetches = []
    for h in range(halves):
        for who in teams:
            block = dot(pick_of(h, who), tiles_b[...])
            send[h, who] = block.reshape(team, each, pixels).astype(BF16)
        fetches.append(exchange(send.at[h], arrived.at[h], put_s.at[h], put_r.at[h]))
        fetches[h][0]()
        arrived[h, me] = send[h, me]

    def morph_of(g, f):
        return fit[g, f, 0:width]

    def first_gram(g):
        total = dot_nt(morph_of(g, 0), morph_of(g, 0))
        for f in range(1, foot):
            total = total + dot_nt(morph_of(g, f), morph_of(g, f))
        total = total * same
        return [(gram, g, total.astype(BF16)), (sed_step, g, wide(sed_stepsize(total)))]

    over_groups(first_gram, 0, groups, 4)

    crew = per_half * foot * span
    crew_row, crew_band_row = split_row((crew, 1), 0, span)
    crew_band_row, crew_member_row = split_row((crew, 1), 0, size)
    crew_band_row = crew_band_row - crew_row * bands
    crew_col, _ = split_row((1, crew), 1, span)
    crew_band_col, crew_member_col = split_row((1, crew), 1, size)
    crew_band_col = crew_band_col - crew_col * bands
    group_row = split_row((crew, 1), 0, foot * span)[0]
    group_col = split_row((1, crew), 1, foot * span)[0]
    foot_row = crew_row - group_row * foot
    foot_col = crew_col - group_col * foot
    entry_row = lanes_of(*[pos_row + f * rows for f in range(foot)])
    entry_col = rows_of(*[pos_col + f * rows for f in range(foot)])
    facts = lanes_of(
        jnp.broadcast_to(source_col, (entries, 128)), jnp.broadcast_to(rank_col, (entries, 128))
    ).astype(BF16)
    facts_t = rows_of(source_row, rank_row, jnp.zeros((6, entries), F32)).astype(BF16)

    def give_of(h, first):
        here = ((h * per_half + group_row) * size + crew_member_row + foot_row * rows).astype(F32)
        found = dot(flag(here == entry_row).astype(BF16), facts)
        at = (found[:, 0:1] - first) * each + found[:, 128:129] + (crew_band_row * held).astype(F32)
        return flag(count_up((crew, crowd), 1) == at).astype(BF16)

    def give_t_of(h, first):
        here = ((h * per_half + group_col) * size + crew_member_col + foot_col * rows).astype(F32)
        found = dot(facts_t, flag(entry_col == here).astype(BF16))
        at = (found[0:1] - first) * each + found[1:2] + (crew_band_col * held).astype(F32)
        return flag(count_up((crowd, crew), 0) == at).astype(BF16)

    def first_seds(g):
        cross = dot_nt(fit[g, 0, width:used], morph_of(g, 0))
        for f in range(1, foot):
            cross = cross + dot_nt(fit[g, f, width:used], morph_of(g, f))
        old = seds[g]
        slope = dot(old.astype(BF16), gram[g]) - cross * same_t
        sed = jnp.maximum(old - slope * every_band(sed_step[g, :, 0:1]), 0.0).astype(BF16)
        return [(seds, g, sed.astype(F32))]

    def plan_move(g):
        sed = seds[g]
        bold = sed.astype(BF16)
        small = dot_nt(bold, bold)
        flat = jnp.sum(small * small, axis=1, keepdims=True).reshape(bands, size, 1)
        step = 1.0 / (jnp.sqrt(jnp.sum(flat, axis=0)) + 1.0)
        blank = jnp.zeros((span, depth - width), F32)
        right = (unit - jnp.concatenate([sed, blank], axis=1)) * every_band(step)
        right = jnp.concatenate([right, lift * (-0.1 * step)], axis=0).astype(BF16)
        left = dot_nt(eye, jnp.concatenate([sed, members], axis=0).astype(BF16)).astype(BF16)
        return [(move, g, dot(left, right).astype(BF16))]

    def moved(g, f):
        shift = dot(move[g], fit[g, f])
        return jnp.maximum(fit[g, f, 0:width].astype(F32) + shift, 0.0).astype(BF16)

    def first_morphs(g):
        return [(fit, (g, f, slice(0, width)), moved(g, f)) for f in range(foot)]

    def second_seds(g):
        total = dot_nt(fit[g, 0, 0:used], morph_of(g, 0))
        for f in range(1, foot):
            total = total + dot_nt(fit[g, f, 0:used], morph_of(g, f))
        cross = total[width:used] * same_t
        total = total[0:width] * same
        old = seds[g]
        slope = dot(old.astype(BF16), total.astype(BF16)) - cross
        sed = jnp.maximum(old - slope * every_band(sed_stepsize(total)), 0.0).astype(BF16)
        return [(seds, g, sed.astype(F32))]

    def last_models(g):
        sed = seds[g].astype(BF16)
        return [(mod, (g, f), dot(sed, moved(g, f)).astype(BF16)) for f in range(foot)]

    trips = []
    for h in range(halves):
        first = h * per_half
        fetches[h][1]()
        block = jnp.zeros((crew, pixels), F32)
        for k, who in enumerate(teams):
            come = arrived[h, who].astype(F32).reshape(crowd, pixels).astype(BF16)
            block = block + dot(give_of(h, k * team), come)
        block = block.astype(BF16).reshape(per_half, foot, span, pixels)
        fit[first : first + per_half, :, width:used] = block
        over_groups(first_seds, first, per_half, 4)
        over_groups(plan_move, first, per_half, 4)
        over_groups(first_morphs, first, per_half, 4)
        over_groups(second_seds, first, per_half, 4)
        over_groups(plan_move, first, per_half, 4)
        over_groups(last_models, first, per_half, 4)
        models = mod[first : first + per_half].reshape(crew, pixels)
        for k, who in enumerate(teams):
            block = dot(give_t_of(h, k * team), models)
            outb[h, who] = block.reshape(team, each, pixels).astype(BF16)
        trips.append(exchange(outb.at[h], ret.at[h], back_s.at[h], back_r.at[h]))
        trips[h][0]()
        ret[h, me] = outb[h, me]

    def put_back(g, placed):
        lean = dot_nt(gather_k, seds[g].astype(BF16))
        return placed + dot(lean.astype(BF16), chosen(g))

    placed = lax.fori_loop(0, groups, put_back, jnp.zeros((comps, bands * rows), F32))
    for b in range(bands):
        sed_out[b] = placed[:, b * rows : (b + 1) * rows].astype(BF16)

    for h in range(halves):
        trips[h][1]()
        total = jnp.zeros((stock, pixels), F32)
        for who in teams:
            come = ret[h, who].astype(F32).reshape(crowd, pixels).astype(BF16)
            total = total + dot(pick_t_of(h, who), come)
        left = tiles if h == 0 else white
        white[...] = left[...] - total.reshape(bands, tile_rows, pixels)

    squares = jnp.zeros((8, 128), F32)
    for b in range(bands):
        square = white[b] * white[b]
        for r in range(0, tile_rows, 8):
            for c in range(0, pixels, 128):
                squares = squares + square[r : r + 8, c : c + 128]

    own_row = jnp.sum(squares, axis=0, keepdims=True)
    part[...] = own_row

    def share(step, incoming):
        there = lax.rem(my + step, everyone)
        here = lax.rem(my - step + everyone, everyone) if incoming else my
        return pltpu.make_async_remote_copy(
            src_ref=part, dst_ref=parts.at[here], send_sem=sum_s.at[step],
            recv_sem=sum_r.at[step],
            device_id={"grp": lax.div(there, peers), "dev": lax.rem(there, peers)}, device_id_type=MESH,
        )

    def start_share(step, carry):
        share(step, False).start()
        return carry

    def end_share(step, carry):
        share(step, True).wait_recv()
        return carry

    def end_sent(step, carry):
        share(step, False).wait_send()
        return carry

    lax.fori_loop(1, everyone, start_share, 0)
    parts[my] = own_row
    ask_out()
    for trip in fetches + trips:
        trip[2]()
    lax.fori_loop(1, everyone, end_share, 0)
    total = jnp.sum(parts[...], axis=0)
    total = jnp.sum(jnp.sum(total, axis=1, keepdims=True), axis=0, keepdims=True)
    count_all = float(bands * tile_rows * pixels * everyone)
    scale_out[...] = jnp.broadcast_to(1.0 / jnp.sqrt(total / count_all + 1e-06), (8, 128))
    lax.fori_loop(1, everyone, end_sent, 0)


def on_device(pixel_tiles, blend_source, blend_slot, component_count, sed_start, morph_start):
    peers = lax.axis_size("dev")
    regions = lax.axis_size("grp")
    rows, foot = blend_source.shape
    tile_rows, bands, pixels = pixel_tiles.shape
    comps = sed_start.shape[1]
    size = math.gcd(rows, 8)
    groups = rows // size
    halves, held = plan_slots(peers, rows, foot, bands, groups)
    width = size * comps
    span = size * bands
    depth = tgt_depth(width, span)
    vmem = pl.BlockSpec(memory_space=pltpu.VMEM)
    hbm = pl.BlockSpec(memory_space=pl.ANY)
    dma = pltpu.SemaphoreType.DMA
    parcel = pltpu.VMEM((halves, peers, bands * held, pixels), BF16)
    residual, sed_final, scale = pl.pallas_call(
        functools.partial(kernel, peers, regions, halves, held, size),
        out_shape=(
            jax.ShapeDtypeStruct((bands, tile_rows, pixels), F32),
            jax.ShapeDtypeStruct((bands, comps, rows), BF16),
            jax.ShapeDtypeStruct((8, 128), F32),
        ),
        in_specs=[hbm] + [vmem] * 4 + [hbm],
        out_specs=(vmem, vmem, vmem),
        scratch_shapes=[
            pltpu.VMEM((bands, tile_rows, pixels), F32),
            pltpu.VMEM((bands * tile_rows, pixels), BF16),
            pltpu.VMEM(morph_start.shape, BF16),
            pltpu.VMEM((groups, foot, depth, pixels), BF16),
            pltpu.VMEM((groups, width, width), BF16),
            pltpu.VMEM((groups, span, width), F32),
            pltpu.VMEM((groups, size, 128), F32),
            pltpu.VMEM((groups, width, depth), BF16),
            pltpu.VMEM((groups, foot, span, pixels), BF16),
            pltpu.VMEM((8, 128), jnp.int32),
            pltpu.SMEM((8, 128), jnp.int32),
            pltpu.VMEM((peers, 1, 128), F32),
            pltpu.VMEM((peers, 1, 128), F32),
            parcel,
            parcel,
            parcel,
            parcel,
            pltpu.VMEM((1, 128), F32),
            pltpu.VMEM((peers * regions, 1, 128), F32),
            dma((3,)),
            dma((peers,)),
            dma((peers,)),
            dma((halves, peers)),
            dma((halves, peers)),
            dma((halves, peers)),
            dma((halves, peers)),
            dma((peers * regions,)),
            dma((peers * regions,)),
        ],
        compiler_params=pltpu.CompilerParams(
            collective_id=0, has_side_effects=True, vmem_limit_bytes=60 * 1024 * 1024
        ),
    )(
        jnp.transpose(pixel_tiles, (1, 0, 2)),
        jnp.transpose(blend_source),
        jnp.transpose(blend_slot),
        component_count.reshape(1, rows),
        jnp.transpose(sed_start, (2, 1, 0)),
        morph_start,
    )
    white = residual * scale[0, 0]
    return jnp.transpose(white, (1, 0, 2)), jnp.transpose(sed_final, (2, 1, 0))


def solution(mesh):
    placed = (
        P(("grp", "dev"), None, None),
        P(("grp", "dev"), None),
        P(("grp", "dev"), None),
        P(("grp", "dev")),
        P(("grp", "dev"), None, None),
        P(("grp", "dev"), None, None, None),
    )
    return jax.shard_map(
        on_device,
        mesh=mesh,
        in_specs=placed,
        out_specs=(P(("grp", "dev"), None, None), P(("grp", "dev"), None, None)),
        check_vma=False,
    )
```

time: 74 us -> 64.5 us (0.87)
  Pallas kernels: 67.8 us -> 58.2 us
    pallas_call x1, Pallas kernels: 67.8 us -> 58.2 us  [on_device(): pl.pallas_call(functools.partial(kernel, peers, regions, halves, held, si...]
where the time goes in v2:
time: 64.5 us; the launch traced here: 64.2 us
  Pallas kernels  58.2 us (90%)
  other arithmetic  2.75 us (4%)
  local copies, waits for them, and re-layouts  2.57 us (4%)
    pallas_call x1, Pallas kernels, on_device(): pl.pallas_call(functools.partial(kernel, peers, regions, halves, held, si...  58.2 us
    transpose x1, other arithmetic, on_device(): jnp.transpose(white, (1, 0, 2))  2.75 us
    unnamed x1, local copies, waits for them, and re-layouts  1.39 us

profile of v2, /device:TPU:0, one launch (start us, length us, event | category | flops | bytes accessed | tf_op | source)
XLA Modules:
  0.0 64.2 jit_solution(13077409888854776143)
XLA Ops:
  0.6 58.2 %shard_map.77 = (f32[6,64,512]{2,1,0:T(8,128)}, bf16[6,24,64]{2,1,0:T(8,128)(2,1)}, f32[8,128]{1,0:T(8,128)}) custom-call(f32[6,64,512]{2,1,0:T(8,128)} %bitcast.9, s32[2,64]{1,0:T(2,128)} %bitcast.12, s32[2,64]{1,0:T(2,128)} %bitcast.13, s32[1,64]{1,0:T(1,128)} %bitcast.14, bf16[6,24,64]{2,1,0:T(8,128)(2,1)} %bitcast.10, bf16[64,2,24,512]{3,2,1,0:T(8,128)(2,1)} %morph_hbm.1), custom_call_target="tpu_custom_call" | custom-call | tf_op jit(solution)/shard_map/pallas_call | solution.py:505
  58.9 1.2 %slice.3 = f32[1,1]{1,0:T(1,128)} slice(f32[8,128]{1,0:T(8,128)} %get-tuple-element.6), slice={[0:1], [0:1]} | slice | bytes 8 | tf_op jit(solution)/shard_map/slice | solution.py:555
  60.1 2.7 %multiply_bitcast_fusion = f32[64,6,512]{2,0,1:T(8,128)} fusion(f32[6,64,512]{2,1,0:T(8,128)} %get-tuple-element.5, f32[]{:T(128)} %bitcast.5), kind=kLoop, calls=%fused_computation | loop fusion | flops 196608 | bytes 1572868 | tf_op jit(solution)/shard_map/transpose | solution.py:556
  62.8 1.4 %copy.9 = bf16[64,24,6]{0,1,2:T(8,128)(2,1)} copy(bf16[64,24,6]{0,1,2:T(8,128)(2,1)} %bitcast.11) | data formatting | bytes 36864

commit v3 on v2

--- a/solution.py
+++ b/solution.py
@@ -105,8 +105,9 @@
 
 
 def kernel(
-    peers, regions, halves, held, size, tiles_hbm, source, slot, count, sed0, morph_hbm, white, sed_out, scale_out,
-    tiles, tiles_b, morph_in, fit, gram, seds, sed_step, move, mod, order_v, order_s, req, wanted, send, arrived, outb, ret, part, parts,
+    peers, regions, halves, held, size,
+    tiles_hbm, source_hbm, slot_hbm, count_hbm, sed_hbm, morph_hbm, white_out, sed_out, scale_out, source, slot, count, sed0,
+    white, sed_made, tiles, tiles_b, morph_in, fit, gram, seds, sed_step, move, mod, give, give_t, pick_t, order_v, order_s, req, wanted, send, arrived, outb, ret, part, parts,
     in_sem, ask_s, ask_r, put_s, put_r, back_s, back_r, sum_s, sum_r,
 ):
     bands, tile_rows, pixels = tiles.shape
@@ -117,6 +118,14 @@
     me = lax.axis_index("dev")
     everyone = peers * regions
     my = lax.axis_index("grp") * peers + me
+    small = [
+        pltpu.make_async_copy(given, kept, in_sem.at[3 + i])
+        for i, (given, kept) in enumerate(
+            ((source_hbm, source), (slot_hbm, slot), (count_hbm, count), (sed_hbm, sed0))
+        )
+    ]
+    for copy in small:
+        copy.start()
     load_tiles = pltpu.make_async_copy(tiles_hbm, tiles, in_sem.at[0])
     load_tiles.start()
     load = pltpu.make_async_copy(morph_hbm, morph_in, in_sem.at[1])
@@ -133,6 +142,8 @@
 
     lax.fori_loop(1, everyone, greet, 0)
 
+    small[0].wait()
+    small[1].wait()
     entries = foot * rows
     source_row = lanes_of(*[source[f : f + 1, :] for f in range(foot)]).astype(F32)
     slot_row = lanes_of(*[slot[f : f + 1, :] for f in range(foot)]).astype(F32)
@@ -210,6 +221,8 @@
     to_scalars = pltpu.make_async_copy(order_v, order_s, in_sem.at[2])
     to_scalars.start()
 
+    small[2].wait()
+    small[3].wait()
     width = size * comps
     span = size * bands
     used = width + span
@@ -399,7 +412,12 @@
 
     def last_models(g):
         sed = seds[g].astype(BF16)
-        return [(mod, (g, f), dot(sed, moved(g, f)).astype(BF16)) for f in range(foot)]
+        return [(mod, (g, f), dot(sed, morph_of(g, f)).astype(BF16)) for f in range(foot)]
+
+    for h in range(halves):
+        for k in range(len(teams)):
+            give[h, k] = give_of(h, k * team)
+            give_t[h, k] = give_t_of(h, k * team)
 
     trips = []
     for h in range(halves):
@@ -408,7 +426,7 @@
         block = jnp.zeros((crew, pixels), F32)
         for k, who in enumerate(teams):
             come = arrived[h, who].astype(F32).reshape(crowd, pixels).astype(BF16)
-            block = block + dot(give_of(h, k * team), come)
+            block = block + dot(give[h, k], come)
         block = block.astype(BF16).reshape(per_half, foot, span, pixels)
         fit[first : first + per_half, :, width:used] = block
         over_groups(first_seds, first, per_half, 4)
@@ -416,10 +434,11 @@
         over_groups(first_morphs, first, per_half, 4)
         over_groups(second_seds, first, per_half, 4)
         over_groups(plan_move, first, per_half, 4)
+        over_groups(first_morphs, first, per_half, 4)
         over_groups(last_models, first, per_half, 4)
         models = mod[first : first + per_half].reshape(crew, pixels)
         for k, who in enumerate(teams):
-            block = dot(give_t_of(h, k * team), models)
+            block = dot(give_t[h, k], models)
             outb[h, who] = block.reshape(team, each, pixels).astype(BF16)
         trips.append(exchange(outb.at[h], ret.at[h], back_s.at[h], back_r.at[h]))
         trips[h][0]()
@@ -429,19 +448,26 @@
         lean = dot_nt(gather_k, seds[g].astype(BF16))
         return placed + dot(lean.astype(BF16), chosen(g))
 
+    for h in range(halves):
+        for k, who in enumerate(teams):
+            pick_t[h, k] = pick_t_of(h, who)
     placed = lax.fori_loop(0, groups, put_back, jnp.zeros((comps, bands * rows), F32))
     for b in range(bands):
-        sed_out[b] = placed[:, b * rows : (b + 1) * rows].astype(BF16)
+        sed_made[b] = placed[:, b * rows : (b + 1) * rows].astype(BF16)
+    keep_sed = pltpu.make_async_copy(sed_made, sed_out, in_sem.at[0])
+    keep_sed.start()
 
     for h in range(halves):
         trips[h][1]()
         total = jnp.zeros((stock, pixels), F32)
-        for who in teams:
+        for k, who in enumerate(teams):
             come = ret[h, who].astype(F32).reshape(crowd, pixels).astype(BF16)
-            total = total + dot(pick_t_of(h, who), come)
+            total = total + dot(pick_t[h, k], come)
         left = tiles if h == 0 else white
         white[...] = left[...] - total.reshape(bands, tile_rows, pixels)
 
+    keep_white = pltpu.make_async_copy(white, white_out, in_sem.at[1])
+    keep_white.start()
     squares = jnp.zeros((8, 128), F32)
     for b in range(bands):
         square = white[b] * white[b]
@@ -484,6 +510,13 @@
     count_all = float(bands * tile_rows * pixels * everyone)
     scale_out[...] = jnp.broadcast_to(1.0 / jnp.sqrt(total / count_all + 1e-06), (8, 128))
     lax.fori_loop(1, everyone, end_sent, 0)
+    keep_sed.wait()
+    keep_white.wait()
+
+
+def finish(scale, residual, sed, white_out, sed_out):
+    white_out[...] = residual[...] * scale[0:1, 0:1]
+    sed_out[...] = sed[...]
 
 
 def on_device(pixel_tiles, blend_source, blend_slot, component_count, sed_start, morph_start):
@@ -501,6 +534,9 @@
     vmem = pl.BlockSpec(memory_space=pltpu.VMEM)
     hbm = pl.BlockSpec(memory_space=pl.ANY)
     dma = pltpu.SemaphoreType.DMA
+    team = math.gcd(peers, 16)
+    crowd = team * bands * held
+    crew = groups // halves * foot * span
     parcel = pltpu.VMEM((halves, peers, bands * held, pixels), BF16)
     residual, sed_final, scale = pl.pallas_call(
         functools.partial(kernel, peers, regions, halves, held, size),
@@ -509,9 +545,15 @@
             jax.ShapeDtypeStruct((bands, comps, rows), BF16),
             jax.ShapeDtypeStruct((8, 128), F32),
         ),
-        in_specs=[hbm] + [vmem] * 4 + [hbm],
-        out_specs=(vmem, vmem, vmem),
+        in_specs=[hbm] * 6,
+        out_specs=(hbm, hbm, vmem),
         scratch_shapes=[
+            pltpu.VMEM((foot, rows), jnp.int32),
+            pltpu.VMEM((foot, rows), jnp.int32),
+            pltpu.VMEM((1, rows), jnp.int32),
+            pltpu.VMEM((bands, comps, rows), BF16),
+            pltpu.VMEM((bands, tile_rows, pixels), F32),
+            pltpu.VMEM((bands, comps, rows), BF16),
             pltpu.VMEM((bands, tile_rows, pixels), F32),
             pltpu.VMEM((bands * tile_rows, pixels), BF16),
             pltpu.VMEM(morph_start.shape, BF16),
@@ -521,6 +563,9 @@
             pltpu.VMEM((groups, size, 128), F32),
             pltpu.VMEM((groups, width, depth), BF16),
             pltpu.VMEM((groups, foot, span, pixels), BF16),
+            pltpu.VMEM((halves, peers // team, crew, crowd), BF16),
+            pltpu.VMEM((halves, peers // team, crowd, crew), BF16),
+            pltpu.VMEM((halves, peers // team, bands * tile_rows, crowd), BF16),
             pltpu.VMEM((8, 128), jnp.int32),
             pltpu.SMEM((8, 128), jnp.int32),
             pltpu.VMEM((peers, 1, 128), F32),
@@ -531,7 +576,7 @@
             parcel,
             pltpu.VMEM((1, 128), F32),
             pltpu.VMEM((peers * regions, 1, 128), F32),
-            dma((3,)),
+            dma((7,)),
             dma((peers,)),
             dma((peers,)),
             dma((halves, peers)),
@@ -542,17 +587,31 @@
             dma((peers * regions,)),
         ],
         compiler_params=pltpu.CompilerParams(
-            collective_id=0, has_side_effects=True, vmem_limit_bytes=60 * 1024 * 1024
+            collective_id=0, has_side_effects=True, vmem_limit_bytes=40 * 1024 * 1024
         ),
     )(
-        jnp.transpose(pixel_tiles, (1, 0, 2)),
-        jnp.transpose(blend_source),
-        jnp.transpose(blend_slot),
-        component_count.reshape(1, rows),
-        jnp.transpose(sed_start, (2, 1, 0)),
-        morph_start,
+        *[
+            pltpu.with_memory_space_constraint(given, pltpu.HBM)
+            for given in (
+                jnp.transpose(pixel_tiles, (1, 0, 2)),
+                jnp.transpose(blend_source),
+                jnp.transpose(blend_slot),
+                component_count.reshape(1, rows),
+                jnp.transpose(sed_start, (2, 1, 0)),
+                morph_start,
+            )
+        ]
     )
-    white = residual * scale[0, 0]
+    white, sed_final = pl.pallas_call(
+        finish,
+        out_shape=(
+            jax.ShapeDtypeStruct((bands, tile_rows, pixels), F32),
+            jax.ShapeDtypeStruct((bands, comps, rows), BF16),
+        ),
+        in_specs=[vmem, vmem, vmem],
+        out_specs=(vmem, vmem),
+        compiler_params=pltpu.CompilerParams(vmem_limit_bytes=8 * 1024 * 1024),
+    )(scale, residual, sed_final)
     return jnp.transpose(white, (1, 0, 2)), jnp.transpose(sed_final, (2, 1, 0))
 
 

time: 64.5 us -> 58.8 us (0.912)
  other arithmetic: 2.75 us -> 0 us
  local copies, waits for them, and re-layouts: 2.57 us -> 0 us
    transpose x1 -> x0, other arithmetic: 2.75 us -> none  [on_device(): jnp.transpose(white, (1, 0, 2))]
    unnamed x1 -> x0, local copies, waits for them, and re-layouts: 1.39 us -> none
    pallas_call x1, Pallas kernels: 58.2 us -> 57 us  [on_device(): pl.pallas_call(functools.partial(kernel, peers, regions, halves, held, si...]
    slice x1 -> x0, local copies, waits for them, and re-layouts: 1.19 us -> none  [on_device(): white = residual * scale[0, 0]]
    pallas_call x0 -> x1, Pallas kernels: none -> 0.97 us  [on_device(): pl.pallas_call(finish, out_shape=(jax.ShapeDtypeStruct((bands, tile_rows,...]
where the time goes in v3:
time: 58.8 us; the launch traced here: 58.6 us
  Pallas kernels  58 us (99%)
  between operations  0.64 us (1%)
    pallas_call x1, Pallas kernels, on_device(): pl.pallas_call(functools.partial(kernel, peers, regions, halves, held, si...  57 us

profile of v3, /device:TPU:0, one launch (start us, length us, event | category | flops | bytes accessed | tf_op | source)
XLA Modules:
  0.0 58.6 jit_solution(3461993874889583372)
XLA Ops:
  0.6 57.0 %shard_map.77 = (f32[6,64,512]{2,1,0:T(8,128)S(1)}, bf16[6,24,64]{2,1,0:T(8,128)(2,1)S(1)}, f32[8,128]{1,0:T(8,128)S(1)}) custom-call(f32[6,64,512]{2,1,0:T(8,128)} %bitcast.7, s32[2,64]{1,0:T(2,128)} %bitcast.9, s32[2,64]{1,0:T(2,128)} %bitcast.10, s32[1,64]{1,0:T(1,128)} %bitcast.11, bf16[6,24,64]{2,1,0:T(8,128)(2,1)} %bitcast.8, ...), custom_call_target="tpu_custom_call" | custom-call | tf_op jit(solution)/shard_map/pallas_call | solution.py:541
  57.7 1.0 %shard_map.78 = (f32[6,64,512]{2,1,0:T(8,128)}, bf16[6,24,64]{2,1,0:T(8,128)(2,1)}) custom-call(f32[8,128]{1,0:T(8,128)S(1)} %get-tuple-element.7.scale, f32[6,64,512]{2,1,0:T(8,128)S(1)} %get-tuple-element.8.residual, bf16[6,24,64]{2,1,0:T(8,128)(2,1)S(1)} %get-tuple-element.9.sed), custom_call_target="tpu_custom_call" | custom-call | tf_op jit(solution)/shard_map/pallas_call | solution.py:605

commit v4 on v3

--- a/solution.py
+++ b/solution.py
@@ -178,36 +178,43 @@
     req[...] = dot(named.astype(BF16), asked.astype(BF16)).reshape(peers, 1, 128)
     pl.semaphore_wait(barrier, everyone - 1)
 
+    planes = 4 if peers % 4 == 0 else 1
+    deck = peers // planes
+    level = lax.div(me, deck)
+    spot = lax.rem(me, deck)
+    upper = lax.div(level, 2)
+    if planes == 4:
+        decks = [2 - upper, 3 - 3 * upper, 4 * upper + 1 - level, level]
+    else:
+        decks = [level]
+
+    def member(c, j):
+        return decks[c] * deck + lax.rem(spot + j, deck)
+
     def exchange(src, dst, send_sem, recv_sem):
-        def copy(step, incoming):
-            there = lax.rem(me + step, peers)
-            here = lax.rem(me - step + peers, peers) if incoming else me
+        def copy(there, here):
             return pltpu.make_async_remote_copy(
                 src_ref=src.at[there], dst_ref=dst.at[here],
-                send_sem=send_sem.at[step], recv_sem=recv_sem.at[step],
+                send_sem=send_sem.at[there], recv_sem=recv_sem.at[here],
                 device_id={"dev": there}, device_id_type=MESH,
             )
 
-        def start():
-            def body(step, carry):
-                copy(step, False).start()
-                return carry
-
-            lax.fori_loop(1, peers, body, 0)
-
-        def wait_in():
-            def body(step, carry):
-                copy(step, True).wait_recv()
-                return carry
-
-            lax.fori_loop(1, peers, body, 0)
-
-        def wait_out():
-            def body(step, carry):
-                copy(step, False).wait_send()
-                return carry
-
-            lax.fori_loop(1, peers, body, 0)
+        def each_of(act, classes):
+            for c in classes:
+                def body(j, carry, c=c):
+                    act(member(c, j))
+                    return carry
+
+                lax.fori_loop(1 if c == planes - 1 else 0, deck, body, 0)
+
+        def start(classes=range(planes)):
+            each_of(lambda there: copy(there, me).start(), classes)
+
+        def wait_in(classes=range(planes)):
+            each_of(lambda here: copy(here, here).wait_recv(), classes)
+
+        def wait_out(classes=range(planes)):
+            each_of(lambda there: copy(there, me).wait_send(), classes)
 
         return start, wait_in, wait_out
 
@@ -297,19 +304,20 @@
     crowd = team * each
     stock = bands * tile_rows
     teams = [slice(k, k + team) for k in range(0, peers, team)]
-    _, seat_row = split_row((crowd, 1), 0, each)
-    seat_band_row, seat_rank_row = split_row((crowd, 1), 0, held)
-    peer_col, seat_col = split_row((1, crowd), 1, each)
-    seat_band_row = seat_band_row - split_row((crowd, 1), 0, each)[0] * bands
+    peer_col = split_row((1, crowd), 1, each)[0]
     seat_band_col, seat_rank_col = split_row((1, crowd), 1, held)
     seat_band_col = seat_band_col - peer_col * bands
 
-    def pick_of(h, who):
-        lines = jnp.broadcast_to(wanted[who], (team, each, 128)).reshape(crowd, 128)
-        seat = flag(iota((crowd, 128), 1) == h * held + seat_rank_row)
+    ranks = deck * each
+    asker_row, seat_rank_row = split_row((ranks, 1), 0, held)
+    seat_band_row = asker_row - split_row((ranks, 1), 0, each)[0] * bands
+
+    def pick_of(h, c):
+        lines = rows_of(*[jnp.broadcast_to(wanted[member(c, j)], (each, 128)) for j in range(deck)])
+        seat = flag(iota((ranks, 128), 1) == h * held + seat_rank_row)
         tile = jnp.sum(lines * seat, axis=1, keepdims=True)
         at = jnp.where(tile > 0.0, tile - 1.0 + (seat_band_row * tile_rows).astype(F32), -1.0)
-        return flag(count_up((crowd, stock), 1) == at).astype(BF16)
+        return flag(count_up((ranks, stock), 1) == at).astype(BF16)
 
     def pick_t_of(h, who):
         lines = wanted[who].reshape(team, 128).astype(BF16)
@@ -319,14 +327,17 @@
         at = jnp.where(tile > 0.0, tile - 1.0 + (seat_band_col * tile_rows).astype(F32), -1.0)
         return flag(count_up((stock, crowd), 0) == at).astype(BF16)
 
-    ask_in()
-    fetches = []
+    fetches = [
+        exchange(send.at[h], arrived.at[h], put_s.at[h], put_r.at[h]) for h in range(halves)
+    ]
     for h in range(halves):
-        for who in teams:
-            block = dot(pick_of(h, who), tiles_b[...])
-            send[h, who] = block.reshape(team, each, pixels).astype(BF16)
-        fetches.append(exchange(send.at[h], arrived.at[h], put_s.at[h], put_r.at[h]))
-        fetches[h][0]()
+        for c in range(planes):
+            if h == 0:
+                ask_in([c])
+            block = dot(pick_of(h, c), tiles_b[...]).astype(BF16)
+            for j in range(deck):
+                send[h, member(c, j)] = block[j * each : (j + 1) * each]
+            fetches[h][0]([c])
         arrived[h, me] = send[h, me]
 
     def morph_of(g, f):
@@ -478,13 +489,14 @@
     own_row = jnp.sum(squares, axis=0, keepdims=True)
     part[...] = own_row
 
+    place_of = me * regions + lax.axis_index("grp")
+
     def share(step, incoming):
-        there = lax.rem(my + step, everyone)
-        here = lax.rem(my - step + everyone, everyone) if incoming else my
+        other = step + (step >= place_of).astype(jnp.int32)
         return pltpu.make_async_remote_copy(
-            src_ref=part, dst_ref=parts.at[here], send_sem=sum_s.at[step],
-            recv_sem=sum_r.at[step],
-            device_id={"grp": lax.div(there, peers), "dev": lax.rem(there, peers)}, device_id_type=MESH,
+            src_ref=part, dst_ref=parts.at[other if incoming else place_of], send_sem=sum_s.at[other],
+            recv_sem=sum_r.at[other if incoming else place_of],
+            device_id={"grp": lax.rem(other, regions), "dev": lax.div(other, regions)}, device_id_type=MESH,
         )
 
     def start_share(step, carry):
@@ -499,17 +511,17 @@
         share(step, False).wait_send()
         return carry
 
-    lax.fori_loop(1, everyone, start_share, 0)
-    parts[my] = own_row
+    lax.fori_loop(0, everyone - 1, start_share, 0)
+    parts[place_of] = own_row
     ask_out()
     for trip in fetches + trips:
         trip[2]()
-    lax.fori_loop(1, everyone, end_share, 0)
+    lax.fori_loop(0, everyone - 1, end_share, 0)
     total = jnp.sum(parts[...], axis=0)
     total = jnp.sum(jnp.sum(total, axis=1, keepdims=True), axis=0, keepdims=True)
     count_all = float(bands * tile_rows * pixels * everyone)
     scale_out[...] = jnp.broadcast_to(1.0 / jnp.sqrt(total / count_all + 1e-06), (8, 128))
-    lax.fori_loop(1, everyone, end_sent, 0)
+    lax.fori_loop(0, everyone - 1, end_sent, 0)
     keep_sed.wait()
     keep_white.wait()
 

time: 58.8 us -> 56.1 us (0.954)
  Pallas kernels: 58 us -> 55.3 us
    pallas_call x1, Pallas kernels: 57 us -> 54.3 us  [on_device(): pl.pallas_call(functools.partial(kernel, peers, regions, halves, held, si...]
where the time goes in v4:
time: 56.1 us; the launch traced here: 55.9 us
  Pallas kernels  55.3 us (99%)
  between operations  0.64 us (1%)
    pallas_call x1, Pallas kernels, on_device(): pl.pallas_call(functools.partial(kernel, peers, regions, halves, held, si...  54.3 us

profile of v4, /device:TPU:0, one launch (start us, length us, event | category | flops | bytes accessed | tf_op | source)
XLA Modules:
  0.0 55.9 jit_solution(7734124268563012861)
XLA Ops:
  0.6 54.3 %shard_map.77 = (f32[6,64,512]{2,1,0:T(8,128)S(1)}, bf16[6,24,64]{2,1,0:T(8,128)(2,1)S(1)}, f32[8,128]{1,0:T(8,128)S(1)}) custom-call(f32[6,64,512]{2,1,0:T(8,128)} %bitcast.7, s32[2,64]{1,0:T(2,128)} %bitcast.9, s32[2,64]{1,0:T(2,128)} %bitcast.10, s32[1,64]{1,0:T(1,128)} %bitcast.11, bf16[6,24,64]{2,1,0:T(8,128)(2,1)} %bitcast.8, ...), custom_call_target="tpu_custom_call" | custom-call | tf_op jit(solution)/shard_map/pallas_call | solution.py:553
  55.0 1.0 %shard_map.78 = (f32[6,64,512]{2,1,0:T(8,128)}, bf16[6,24,64]{2,1,0:T(8,128)(2,1)}) custom-call(f32[8,128]{1,0:T(8,128)S(1)} %get-tuple-element.7.scale, f32[6,64,512]{2,1,0:T(8,128)S(1)} %get-tuple-element.8.residual, bf16[6,24,64]{2,1,0:T(8,128)(2,1)S(1)} %get-tuple-element.9.sed), custom_call_target="tpu_custom_call" | custom-call | tf_op jit(solution)/shard_map/pallas_call | solution.py:617

commit v5 on v4

--- a/solution.py
+++ b/solution.py
@@ -64,49 +64,57 @@
     return halves, held
 
 
-def partners(col, row, before, after):
+def turn(*lines):
+    n = lines[0].shape[1]
+    return jnp.transpose(rows_of(*lines, jnp.zeros((8 - len(lines), n), F32)))
+
+
+def partners(col, row):
+    shape = (col.shape[0], row.shape[1])
+    here, there = iota(shape, 0), iota(shape, 1)
     alike = flag(col == row)
-    rank_col = jnp.sum(alike * before, axis=1, keepdims=True)
-    rank_row = jnp.sum(alike * after, axis=0, keepdims=True)
+    rank_col = jnp.sum(alike * flag(there < here), axis=1, keepdims=True)
+    rank_row = jnp.sum(alike * flag(there > here), axis=0, keepdims=True)
     level = flag(jnp.floor(rank_col * 0.5) == jnp.floor(rank_row * 0.5))
-    return alike * level * (before + after)
+    pair = alike * level * flag(here != there)
+    found = jnp.sum(pair * here.astype(F32), axis=0, keepdims=True)
+    return jnp.broadcast_to(found, (8, shape[1])).astype(jnp.int32)
+
+
+def follow(values, at):
+    return jnp.take_along_axis(values, at, axis=1)
+
+
+def lowest(step, length):
+    least = iota(step.shape, 1)
+    reach = 1
+    while reach < length:
+        least = jnp.minimum(least, follow(least, step))
+        step = follow(step, step)
+        reach = reach * 2
+    return least
 
 
 def halve(source_col, source_row, n):
-    entries = 2 * n
-    before = flag(iota((entries, entries), 1) < iota((entries, entries), 0))
-    after = flag(iota((entries, entries), 1) > iota((entries, entries), 0))
-    pair = partners(source_col, source_row, before, after)
-    step = rows_of(pair[n:], pair[:n]).astype(BF16)
-    least = count_up((entries, entries), 0)
-    reach = 1
-    while reach < n:
-        both = dot(step, lanes_of(step, least.astype(BF16)))
-        least = jnp.minimum(least, both[:, entries:])
-        step = both[:, :entries].astype(BF16)
-        reach = reach * 2
-    tail = (least[:n] < least[n:])[:, 0:1]
-    tail_col = jnp.where(tail, source_col[:n], source_col[n:])
-    head_col = jnp.where(tail, source_col[n:], source_col[:n])
-    lane = iota((n, 128), 1)
-    turned = jnp.transpose(jnp.where(lane == 0, tail_col, jnp.where(lane == 1, head_col, 0.0)))
-    before = before[:n, :n]
-    after = after[:n, :n]
-    tails = partners(tail_col, turned[0:1], before, after).astype(BF16)
-    heads = partners(head_col, turned[1:2], before, after).astype(BF16)
-    step = dot(tails, heads).astype(BF16)
-    least = count_up((n, n), 0)
-    reach = 1
-    while reach < n // 2:
-        least = jnp.minimum(least, dot(step, least.astype(BF16)))
-        step = dot(step, step).astype(BF16)
-        reach = reach * 2
-    return flag(least >= dot(tails, least.astype(BF16)))
+    def swap(values):
+        return jnp.concatenate([values[:, n:], values[:, :n]], axis=1)
+
+    least = lowest(swap(partners(source_col, source_row)), n)
+    tail = (least < swap(least))[0:1]
+    other_row = swap(source_row)
+    tail_row = jnp.where(tail, source_row, other_row)
+    head_row = jnp.where(tail, other_row, source_row)
+    turned = turn(tail_row, head_row)[:n]
+    lane = iota((n, 2 * n), 1)
+    tails = partners(turned[:, 0:1], jnp.where(lane[0:1] < n, tail_row, -1.0))
+    heads = partners(turned[:, 1:2], jnp.where(lane[0:1] < n, head_row, -1.0))
+    least = lowest(follow(heads, tails), n // 2)
+    return flag(least >= follow(least, tails))[0:1]
 
 
 def kernel(
     peers, regions, halves, held, size,
-    tiles_hbm, source_hbm, slot_hbm, count_hbm, sed_hbm, morph_hbm, white_out, sed_out, scale_out, source, slot, count, sed0,
+    tiles_hbm, source_hbm, slot_hbm, count_hbm, sed_hbm, morph_hbm, white_out, sed_out, scale_out, scale_made, source, slot, count, sed0,
     white, sed_made, tiles, tiles_b, morph_in, fit, gram, seds, sed_step, move, mod, give, give_t, pick_t, order_v, order_s, req, wanted, send, arrived, outb, ret, part, parts,
     in_sem, ask_s, ask_r, put_s, put_r, back_s, back_r, sum_s, sum_r,
 ):
@@ -147,7 +155,7 @@
     entries = foot * rows
     source_row = lanes_of(*[source[f : f + 1, :] for f in range(foot)]).astype(F32)
     slot_row = lanes_of(*[slot[f : f + 1, :] for f in range(foot)]).astype(F32)
-    turned = jnp.transpose(rows_of(source_row, slot_row, jnp.zeros((6, entries), F32)))
+    turned = turn(source_row, slot_row)
     source_col = turned[:, 0:1]
     slot_col = turned[:, 1:2]
     before = flag(iota((entries, entries), 1) < iota((entries, entries), 0))
@@ -155,8 +163,8 @@
     alike = flag(source_col == source_row)
     if halves == 2:
         half = halve(source_col, source_row, rows)
-        half_col = half[:, 0:1]
-        half_row = jnp.transpose(lanes_of(half, half))[0:1]
+        half_col = turn(half)[:rows, 0:1]
+        half_row = half[:, :rows]
         alone = flag(half_col == half_row)
         base = rows // 2
         pos_col = half_col * base + jnp.sum(alone * before[:rows, :rows], axis=1, keepdims=True)
@@ -192,34 +200,43 @@
         return decks[c] * deck + lax.rem(spot + j, deck)
 
     def exchange(src, dst, send_sem, recv_sem):
-        def copy(there, here):
+        def copy(from_here, to_there, there=me):
             return pltpu.make_async_remote_copy(
-                src_ref=src.at[there], dst_ref=dst.at[here],
-                send_sem=send_sem.at[there], recv_sem=recv_sem.at[here],
-                device_id={"dev": there}, device_id_type=MESH,
+                src_ref=src.at[from_here], dst_ref=dst.at[to_there], send_sem=send_sem,
+                recv_sem=recv_sem, device_id={"dev": there}, device_id_type=MESH,
             )
 
-        def each_of(act, classes):
-            for c in classes:
-                def body(j, carry, c=c):
-                    act(member(c, j))
-                    return carry
-
-                lax.fori_loop(1 if c == planes - 1 else 0, deck, body, 0)
-
-        def start(classes=range(planes)):
-            each_of(lambda there: copy(there, me).start(), classes)
-
-        def wait_in(classes=range(planes)):
-            each_of(lambda here: copy(here, here).wait_recv(), classes)
-
-        def wait_out(classes=range(planes)):
-            each_of(lambda there: copy(there, me).wait_send(), classes)
-
-        return start, wait_in, wait_out
-
-    ask, ask_in, ask_out = exchange(req, wanted, ask_s, ask_r)
-    ask()
+        def start(c):
+            def body(j, carry):
+                there = member(c, j)
+                copy(there, me, there).start()
+                return carry
+
+            lax.fori_loop(1 if c == planes - 1 else 0, deck, body, 0)
+
+        others = pl.ds(0, peers - 1)
+        return start, copy(others, others).wait_recv, copy(others, others).wait_send
+
+    def asking(c, j):
+        there = member(c, j)
+        return pltpu.make_async_remote_copy(
+            src_ref=req.at[there], dst_ref=wanted.at[me], send_sem=ask_s.at[c],
+            recv_sem=ask_r.at[level], device_id={"dev": there}, device_id_type=MESH,
+        )
+
+    def asked_of(c):
+        many = pl.ds(0, deck - 1 if c == planes - 1 else deck)
+        return pltpu.make_async_remote_copy(
+            src_ref=req.at[many], dst_ref=wanted.at[many], send_sem=ask_s.at[c],
+            recv_sem=ask_r.at[decks[c]], device_id={"dev": me}, device_id_type=MESH,
+        )
+
+    for c in range(planes):
+        def ask(j, carry, c=c):
+            asking(c, j).start()
+            return carry
+
+        lax.fori_loop(1 if c == planes - 1 else 0, deck, ask, 0)
     wanted[me] = req[me]
 
     order = jnp.sum(flag(count_up((rows, 128), 1) == pos_col) * count_up((rows, 128), 0), axis=0, keepdims=True)
@@ -276,9 +293,6 @@
 
         lax.fori_loop(0, number // pair, some, 0)
 
-    to_scalars.wait()
-    load.wait()
-
     def begin(g):
         mine = pos_row == (g * size + blend_row).astype(F32)
         kept = jnp.sum(jnp.where(mine, count[...].astype(F32), 0.0), axis=1, keepdims=True)
@@ -295,7 +309,6 @@
             stores.append((fit, (g, f, slice(used, depth)), tail))
         return stores
 
-    over_groups(begin, 0, groups, 2)
     load_tiles.wait()
     tiles_b[...] = tiles[...].reshape(bands * tile_rows, pixels).astype(BF16)
 
@@ -333,11 +346,11 @@
     for h in range(halves):
         for c in range(planes):
             if h == 0:
-                ask_in([c])
+                asked_of(c).wait_recv()
             block = dot(pick_of(h, c), tiles_b[...]).astype(BF16)
             for j in range(deck):
                 send[h, member(c, j)] = block[j * each : (j + 1) * each]
-            fetches[h][0]([c])
+            fetches[h][0](c)
         arrived[h, me] = send[h, me]
 
     def morph_of(g, f):
@@ -350,6 +363,9 @@
         total = total * same
         return [(gram, g, total.astype(BF16)), (sed_step, g, wide(sed_stepsize(total)))]
 
+    to_scalars.wait()
+    load.wait()
+    over_groups(begin, 0, groups, 2)
     over_groups(first_gram, 0, groups, 4)
 
     crew = per_half * foot * span
@@ -452,7 +468,8 @@
             block = dot(give_t[h, k], models)
             outb[h, who] = block.reshape(team, each, pixels).astype(BF16)
         trips.append(exchange(outb.at[h], ret.at[h], back_s.at[h], back_r.at[h]))
-        trips[h][0]()
+        for c in range(planes):
+            trips[h][0](c)
         ret[h, me] = outb[h, me]
 
     def put_back(g, placed):
@@ -491,39 +508,41 @@
 
     place_of = me * regions + lax.axis_index("grp")
 
-    def share(step, incoming):
-        other = step + (step >= place_of).astype(jnp.int32)
+    def share(dev, grp):
         return pltpu.make_async_remote_copy(
-            src_ref=part, dst_ref=parts.at[other if incoming else place_of], send_sem=sum_s.at[other],
-            recv_sem=sum_r.at[other if incoming else place_of],
-            device_id={"grp": lax.rem(other, regions), "dev": lax.div(other, regions)}, device_id_type=MESH,
+            src_ref=part, dst_ref=parts.at[place_of], send_sem=sum_s, recv_sem=sum_r,
+            device_id={"grp": grp, "dev": dev}, device_id_type=MESH,
         )
 
-    def start_share(step, carry):
-        share(step, False).start()
+    def start_share(dev, carry):
+        for grp in range(regions):
+            @pl.when(dev * regions + grp != place_of)
+            def _():
+                share(dev, grp).start()
         return carry
 
-    def end_share(step, carry):
-        share(step, True).wait_recv()
-        return carry
-
-    def end_sent(step, carry):
-        share(step, False).wait_send()
-        return carry
-
-    lax.fori_loop(0, everyone - 1, start_share, 0)
+    many = pl.ds(0, everyone - 1)
+    shares = pltpu.make_async_remote_copy(
+        src_ref=parts.at[many], dst_ref=parts.at[many], send_sem=sum_s, recv_sem=sum_r,
+        device_id={"dev": me}, device_id_type=MESH,
+    )
+    lax.fori_loop(0, peers, start_share, 0)
     parts[place_of] = own_row
-    ask_out()
+    for c in range(planes):
+        asked_of(c).wait_send()
     for trip in fetches + trips:
         trip[2]()
-    lax.fori_loop(0, everyone - 1, end_share, 0)
+    shares.wait_recv()
     total = jnp.sum(parts[...], axis=0)
     total = jnp.sum(jnp.sum(total, axis=1, keepdims=True), axis=0, keepdims=True)
     count_all = float(bands * tile_rows * pixels * everyone)
-    scale_out[...] = jnp.broadcast_to(1.0 / jnp.sqrt(total / count_all + 1e-06), (8, 128))
-    lax.fori_loop(0, everyone - 1, end_sent, 0)
+    scale_made[...] = jnp.broadcast_to(1.0 / jnp.sqrt(total / count_all + 1e-06), (8, 128))
+    keep_scale = pltpu.make_async_copy(scale_made, scale_out, in_sem.at[2])
+    keep_scale.start()
+    shares.wait_send()
     keep_sed.wait()
     keep_white.wait()
+    keep_scale.wait()
 
 
 def finish(scale, residual, sed, white_out, sed_out):
@@ -558,8 +577,9 @@
             jax.ShapeDtypeStruct((8, 128), F32),
         ),
         in_specs=[hbm] * 6,
-        out_specs=(hbm, hbm, vmem),
+        out_specs=(hbm, hbm, hbm),
         scratch_shapes=[
+            pltpu.VMEM((8, 128), F32),
             pltpu.VMEM((foot, rows), jnp.int32),
             pltpu.VMEM((foot, rows), jnp.int32),
             pltpu.VMEM((1, rows), jnp.int32),
@@ -589,14 +609,14 @@
             pltpu.VMEM((1, 128), F32),
             pltpu.VMEM((peers * regions, 1, 128), F32),
             dma((7,)),
-            dma((peers,)),
-            dma((peers,)),
-            dma((halves, peers)),
-            dma((halves, peers)),
-            dma((halves, peers)),
-            dma((halves, peers)),
-            dma((peers * regions,)),
-            dma((peers * regions,)),
+            dma((4,)),
+            dma((4,)),
+            dma((halves,)),
+            dma((halves,)),
+            dma((halves,)),
+            dma((halves,)),
+            dma,
+            dma,
         ],
         compiler_params=pltpu.CompilerParams(
             collective_id=0, has_side_effects=True, vmem_limit_bytes=40 * 1024 * 1024

time: 56.1 us -> 53.2 us (0.948)
  Pallas kernels: 55.3 us -> 52.4 us
    pallas_call x1, Pallas kernels: 54.3 us -> 51.5 us  [on_device(): pl.pallas_call(functools.partial(kernel, peers, regions, halves, held, si...]
where the time goes in v5:
time: 53.2 us; the launch traced here: 53.1 us
  Pallas kernels  52.4 us (98%)
  between operations  0.64 us (1%)
    pallas_call x1, Pallas kernels, on_device(): pl.pallas_call(functools.partial(kernel, peers, regions, halves, held, si...  51.5 us

profile of v5, /device:TPU:0, one launch (start us, length us, event | category | flops | bytes accessed | tf_op | source)
XLA Modules:
  0.0 53.1 jit_solution(9603321017170044873)
XLA Ops:
  0.6 51.5 %shard_map.77 = (f32[6,64,512]{2,1,0:T(8,128)S(1)}, bf16[6,24,64]{2,1,0:T(8,128)(2,1)S(1)}, f32[8,128]{1,0:T(8,128)S(1)}) custom-call(f32[6,64,512]{2,1,0:T(8,128)} %bitcast.7, s32[2,64]{1,0:T(2,128)} %bitcast.9, s32[2,64]{1,0:T(2,128)} %bitcast.10, s32[1,64]{1,0:T(1,128)} %bitcast.11, bf16[6,24,64]{2,1,0:T(8,128)(2,1)} %bitcast.8, ...), custom_call_target="tpu_custom_call" | custom-call | tf_op jit(solution)/shard_map/pallas_call | solution.py:572
  52.1 1.0 %shard_map.78 = (f32[6,64,512]{2,1,0:T(8,128)}, bf16[6,24,64]{2,1,0:T(8,128)(2,1)}) custom-call(f32[8,128]{1,0:T(8,128)S(1)} %get-tuple-element.7.scale, f32[6,64,512]{2,1,0:T(8,128)S(1)} %get-tuple-element.8.residual, bf16[6,24,64]{2,1,0:T(8,128)(2,1)S(1)} %get-tuple-element.9.sed), custom_call_target="tpu_custom_call" | custom-call | tf_op jit(solution)/shard_map/pallas_call | solution.py:637

commit v6 on v5

--- a/solution.py
+++ b/solution.py
@@ -51,6 +51,9 @@
 
 def tgt_depth(width, span):
     return (width + span) // 16 * 16 + 16
+
+
+CUTS = 2
 
 
 def plan_slots(peers, rows, foot, bands, groups):
@@ -125,7 +128,6 @@
     per_half = groups // halves
     me = lax.axis_index("dev")
     everyone = peers * regions
-    my = lax.axis_index("grp") * peers + me
     small = [
         pltpu.make_async_copy(given, kept, in_sem.at[3 + i])
         for i, (given, kept) in enumerate(
@@ -140,15 +142,18 @@
     load.start()
     barrier = pltpu.get_barrier_semaphore()
 
-    def greet(step, carry):
-        other = lax.rem(my + step, everyone)
-        pl.semaphore_signal(
-            barrier, inc=1, device_id={"grp": lax.div(other, peers), "dev": lax.rem(other, peers)},
-            device_id_type=MESH,
-        )
+    place_of = me * regions + lax.axis_index("grp")
+
+    def greet(dev, carry):
+        for grp in range(regions):
+            @pl.when(dev * regions + grp != place_of)
+            def _():
+                pl.semaphore_signal(
+                    barrier, inc=1, device_id={"grp": grp, "dev": dev}, device_id_type=MESH
+                )
         return carry
 
-    lax.fori_loop(1, everyone, greet, 0)
+    lax.fori_loop(0, peers, greet, 0)
 
     small[0].wait()
     small[1].wait()
@@ -206,37 +211,39 @@
                 recv_sem=recv_sem, device_id={"dev": there}, device_id_type=MESH,
             )
 
-        def start(c):
+        def start(c, low=0, high=deck):
             def body(j, carry):
                 there = member(c, j)
                 copy(there, me, there).start()
                 return carry
 
-            lax.fori_loop(1 if c == planes - 1 else 0, deck, body, 0)
+            lax.fori_loop(max(low, 1 if c == planes - 1 else 0), high, body, 0)
 
         others = pl.ds(0, peers - 1)
         return start, copy(others, others).wait_recv, copy(others, others).wait_send
 
-    def asking(c, j):
+    def asking(c, j, facing):
         there = member(c, j)
         return pltpu.make_async_remote_copy(
-            src_ref=req.at[there], dst_ref=wanted.at[me], send_sem=ask_s.at[c],
-            recv_sem=ask_r.at[level], device_id={"dev": there}, device_id_type=MESH,
+            src_ref=req.at[there], dst_ref=wanted.at[me], send_sem=ask_s.at[c, facing],
+            recv_sem=ask_r.at[level, facing], device_id={"dev": there}, device_id_type=MESH,
         )
 
-    def asked_of(c):
-        many = pl.ds(0, deck - 1 if c == planes - 1 else deck)
+    def asked_of(c, facing):
+        many = pl.ds(0, 1 if facing else deck - 1)
         return pltpu.make_async_remote_copy(
-            src_ref=req.at[many], dst_ref=wanted.at[many], send_sem=ask_s.at[c],
-            recv_sem=ask_r.at[decks[c]], device_id={"dev": me}, device_id_type=MESH,
+            src_ref=req.at[many], dst_ref=wanted.at[many], send_sem=ask_s.at[c, facing],
+            recv_sem=ask_r.at[decks[c], facing], device_id={"dev": me}, device_id_type=MESH,
         )
 
     for c in range(planes):
         def ask(j, carry, c=c):
-            asking(c, j).start()
+            asking(c, j, 0).start()
             return carry
 
-        lax.fori_loop(1 if c == planes - 1 else 0, deck, ask, 0)
+        if c < planes - 1:
+            asking(c, 0, 1).start()
+        lax.fori_loop(1, deck, ask, 0)
     wanted[me] = req[me]
 
     order = jnp.sum(flag(count_up((rows, 128), 1) == pos_col) * count_up((rows, 128), 0), axis=0, keepdims=True)
@@ -325,12 +332,13 @@
     asker_row, seat_rank_row = split_row((ranks, 1), 0, held)
     seat_band_row = asker_row - split_row((ranks, 1), 0, each)[0] * bands
 
-    def pick_of(h, c):
-        lines = rows_of(*[jnp.broadcast_to(wanted[member(c, j)], (each, 128)) for j in range(deck)])
-        seat = flag(iota((ranks, 128), 1) == h * held + seat_rank_row)
+    def pick_of(h, c, who):
+        lines = rows_of(*[jnp.broadcast_to(wanted[member(c, j)], (each, 128)) for j in who])
+        n = len(who) * each
+        seat = flag(iota((n, 128), 1) == h * held + seat_rank_row[:n])
         tile = jnp.sum(lines * seat, axis=1, keepdims=True)
-        at = jnp.where(tile > 0.0, tile - 1.0 + (seat_band_row * tile_rows).astype(F32), -1.0)
-        return flag(count_up((ranks, stock), 1) == at).astype(BF16)
+        at = jnp.where(tile > 0.0, tile - 1.0 + (seat_band_row[:n] * tile_rows).astype(F32), -1.0)
+        return flag(count_up((n, stock), 1) == at).astype(BF16)
 
     def pick_t_of(h, who):
         lines = wanted[who].reshape(team, 128).astype(BF16)
@@ -344,13 +352,19 @@
         exchange(send.at[h], arrived.at[h], put_s.at[h], put_r.at[h]) for h in range(halves)
     ]
     for h in range(halves):
-        for c in range(planes):
-            if h == 0:
-                asked_of(c).wait_recv()
-            block = dot(pick_of(h, c), tiles_b[...]).astype(BF16)
-            for j in range(deck):
-                send[h, member(c, j)] = block[j * each : (j + 1) * each]
-            fetches[h][0](c)
+        pieces = [(c, 0, deck) for c in range(planes)]
+        if h == 0 and planes > 1:
+            pieces = [(0, 0, 1), (1, 0, 1), (0, 1, deck), (1, 1, deck)] + pieces[2:]
+        for c, low, high in pieces:
+            if h == 0 and low == 0 and c < planes - 1:
+                asked_of(c, 1).wait_recv()
+            if h == 0 and high > 1:
+                asked_of(c, 0).wait_recv()
+            who = range(low, high)
+            block = dot(pick_of(h, c, who), tiles_b[...]).astype(BF16)
+            for i, j in enumerate(who):
+                send[h, member(c, j)] = block[i * each : (i + 1) * each]
+            fetches[h][0](c, low, high)
         arrived[h, me] = send[h, me]
 
     def morph_of(g, f):
@@ -419,12 +433,16 @@
         left = dot_nt(eye, jnp.concatenate([sed, members], axis=0).astype(BF16)).astype(BF16)
         return [(move, g, dot(left, right).astype(BF16))]
 
-    def moved(g, f):
-        shift = dot(move[g], fit[g, f])
-        return jnp.maximum(fit[g, f, 0:width].astype(F32) + shift, 0.0).astype(BF16)
-
-    def first_morphs(g):
-        return [(fit, (g, f, slice(0, width)), moved(g, f)) for f in range(foot)]
+    def next_morphs(lanes):
+        def body(g):
+            stores = []
+            for f in range(foot):
+                shift = dot(move[g], fit[g, f, :, lanes])
+                new = jnp.maximum(fit[g, f, 0:width, lanes].astype(F32) + shift, 0.0)
+                stores.append((fit, (g, f, slice(0, width), lanes), new.astype(BF16)))
+            return stores
+
+        return body
 
     def second_seds(g):
         total = dot_nt(fit[g, 0, 0:used], morph_of(g, 0))
@@ -437,9 +455,19 @@
         sed = jnp.maximum(old - slope * every_band(sed_stepsize(total)), 0.0).astype(BF16)
         return [(seds, g, sed.astype(F32))]
 
-    def last_models(g):
-        sed = seds[g].astype(BF16)
-        return [(mod, (g, f), dot(sed, morph_of(g, f)).astype(BF16)) for f in range(foot)]
+    def last_models(lanes):
+        def body(g):
+            sed = seds[g].astype(BF16)
+            return [
+                (mod, (g, f, slice(None), lanes), dot(sed, fit[g, f, 0:width, lanes]).astype(BF16))
+                for f in range(foot)
+            ]
+
+        return body
+
+    everything = slice(0, pixels)
+    window = pixels // CUTS
+    cuts = [slice(c * window, (c + 1) * window) for c in range(CUTS)]
 
     for h in range(halves):
         for k in range(len(teams)):
@@ -458,19 +486,20 @@
         fit[first : first + per_half, :, width:used] = block
         over_groups(first_seds, first, per_half, 4)
         over_groups(plan_move, first, per_half, 4)
-        over_groups(first_morphs, first, per_half, 4)
+        over_groups(next_morphs(everything), first, per_half, 4)
         over_groups(second_seds, first, per_half, 4)
         over_groups(plan_move, first, per_half, 4)
-        over_groups(first_morphs, first, per_half, 4)
-        over_groups(last_models, first, per_half, 4)
-        models = mod[first : first + per_half].reshape(crew, pixels)
-        for k, who in enumerate(teams):
-            block = dot(give_t[h, k], models)
-            outb[h, who] = block.reshape(team, each, pixels).astype(BF16)
-        trips.append(exchange(outb.at[h], ret.at[h], back_s.at[h], back_r.at[h]))
-        for c in range(planes):
-            trips[h][0](c)
-        ret[h, me] = outb[h, me]
+        for i, lanes in enumerate(cuts):
+            over_groups(next_morphs(lanes), first, per_half, 4)
+            over_groups(last_models(lanes), first, per_half, 4)
+            models = mod[first : first + per_half, :, :, lanes].reshape(crew, window)
+            for k, who in enumerate(teams):
+                block = dot(give_t[h, k], models)
+                outb[h, i, who] = block.reshape(team, each, window).astype(BF16)
+            trips.append(exchange(outb.at[h, i], ret.at[h, i], back_s.at[h, i], back_r.at[h, i]))
+            for c in range(planes):
+                trips[-1][0](c)
+            ret[h, i, me] = outb[h, i, me]
 
     def put_back(g, placed):
         lean = dot_nt(gather_k, seds[g].astype(BF16))
@@ -485,28 +514,29 @@
     keep_sed = pltpu.make_async_copy(sed_made, sed_out, in_sem.at[0])
     keep_sed.start()
 
+    squares = jnp.zeros((8, 128), F32)
     for h in range(halves):
-        trips[h][1]()
-        total = jnp.zeros((stock, pixels), F32)
-        for k, who in enumerate(teams):
-            come = ret[h, who].astype(F32).reshape(crowd, pixels).astype(BF16)
-            total = total + dot(pick_t[h, k], come)
-        left = tiles if h == 0 else white
-        white[...] = left[...] - total.reshape(bands, tile_rows, pixels)
+        for i, lanes in enumerate(cuts):
+            trips[h * CUTS + i][1]()
+            total = jnp.zeros((stock, window), F32)
+            for k, who in enumerate(teams):
+                come = ret[h, i, who].astype(F32).reshape(crowd, window).astype(BF16)
+                total = total + dot(pick_t[h, k], come)
+            total = total.reshape(bands, tile_rows, window)
+            left = tiles if h == 0 else white
+            for b in range(bands):
+                rest = left[b, :, lanes] - total[b]
+                white[b, :, lanes] = rest
+                if h == halves - 1:
+                    square = rest * rest
+                    for r in range(0, tile_rows, 8):
+                        for c in range(0, window, 128):
+                            squares = squares + square[r : r + 8, c : c + 128]
 
     keep_white = pltpu.make_async_copy(white, white_out, in_sem.at[1])
     keep_white.start()
-    squares = jnp.zeros((8, 128), F32)
-    for b in range(bands):
-        square = white[b] * white[b]
-        for r in range(0, tile_rows, 8):
-            for c in range(0, pixels, 128):
-                squares = squares + square[r : r + 8, c : c + 128]
-
     own_row = jnp.sum(squares, axis=0, keepdims=True)
     part[...] = own_row
-
-    place_of = me * regions + lax.axis_index("grp")
 
     def share(dev, grp):
         return pltpu.make_async_remote_copy(
@@ -529,7 +559,9 @@
     lax.fori_loop(0, peers, start_share, 0)
     parts[place_of] = own_row
     for c in range(planes):
-        asked_of(c).wait_send()
+        asked_of(c, 0).wait_send()
+        if c < planes - 1:
+            asked_of(c, 1).wait_send()
     for trip in fetches + trips:
         trip[2]()
     shares.wait_recv()
@@ -569,6 +601,7 @@
     crowd = team * bands * held
     crew = groups // halves * foot * span
     parcel = pltpu.VMEM((halves, peers, bands * held, pixels), BF16)
+    returned = pltpu.VMEM((halves, CUTS, peers, bands * held, pixels // CUTS), BF16)
     residual, sed_final, scale = pl.pallas_call(
         functools.partial(kernel, peers, regions, halves, held, size),
         out_shape=(
@@ -604,17 +637,17 @@
             pltpu.VMEM((peers, 1, 128), F32),
             parcel,
             parcel,
-            parcel,
-            parcel,
+            returned,
+            returned,
             pltpu.VMEM((1, 128), F32),
             pltpu.VMEM((peers * regions, 1, 128), F32),
             dma((7,)),
-            dma((4,)),
-            dma((4,)),
+            dma((4, 2)),
+            dma((4, 2)),
             dma((halves,)),
             dma((halves,)),
-            dma((halves,)),
-            dma((halves,)),
+            dma((halves, CUTS)),
+            dma((halves, CUTS)),
             dma,
             dma,
         ],

time: 53.2 us -> 52.5 us (0.987)
  Pallas kernels: 52.4 us -> 51.7 us
    pallas_call x1, Pallas kernels: 51.5 us -> 50.7 us  [on_device(): pl.pallas_call(functools.partial(kernel, peers, regions, halves, held, si...]
where the time goes in v6:
time: 52.5 us; the launch traced here: 52.3 us
  Pallas kernels  51.7 us (98%)
  between operations  0.64 us (1%)
    pallas_call x1, Pallas kernels, on_device(): pl.pallas_call(functools.partial(kernel, peers, regions, halves, held, si...  50.7 us

profile of v6, /device:TPU:0, one launch (start us, length us, event | category | flops | bytes accessed | tf_op | source)
XLA Modules:
  0.0 52.3 jit_solution(16030792528785318569)
XLA Ops:
  0.6 50.7 %shard_map.77 = (f32[6,64,512]{2,1,0:T(8,128)S(1)}, bf16[6,24,64]{2,1,0:T(8,128)(2,1)S(1)}, f32[8,128]{1,0:T(8,128)S(1)}) custom-call(f32[6,64,512]{2,1,0:T(8,128)} %bitcast.7, s32[2,64]{1,0:T(2,128)} %bitcast.9, s32[2,64]{1,0:T(2,128)} %bitcast.10, s32[1,64]{1,0:T(1,128)} %bitcast.11, bf16[6,24,64]{2,1,0:T(8,128)(2,1)} %bitcast.8, ...), custom_call_target="tpu_custom_call" | custom-call | tf_op jit(solution)/shard_map/pallas_call | solution.py:605
  51.4 1.0 %shard_map.78 = (f32[6,64,512]{2,1,0:T(8,128)}, bf16[6,24,64]{2,1,0:T(8,128)(2,1)}) custom-call(f32[8,128]{1,0:T(8,128)S(1)} %get-tuple-element.7.scale, f32[6,64,512]{2,1,0:T(8,128)S(1)} %get-tuple-element.8.residual, bf16[6,24,64]{2,1,0:T(8,128)(2,1)S(1)} %get-tuple-element.9.sed), custom_call_target="tpu_custom_call" | custom-call | tf_op jit(solution)/shard_map/pallas_call | solution.py:670
